TPU v7x, 32 devices: a whole 2x2x4 slice. The times are simulated.
32 devices in a mesh: pop: 4 (over y, x), dp: 8 (over z, core).
Axes of the slice: x: 2, y: 2, z: 4, core: 2. Of those that a mesh axis runs over, the one named last changes fastest.
Arguments:
- observations: bfloat16 [4, 4096, 256], P('pop', 'dp'), may hold values from -6 to 6
- returns: float32 [4, 4096], P('pop', 'dp'), may hold values from 0 to 2
- actions: int32 [4, 4096], P('pop', 'dp'), may hold values from 0 to 17
- w_input: bfloat16 [4, 256, 2048], P('pop', 'dp'), may hold values from -0.375 to 0.375
- w_middle: bfloat16 [4, 2048, 2048], P('pop', 'dp'), may hold values from -0.125 to 0.125
- w_head: bfloat16 [4, 2048, 18], P('pop', 'dp'), may hold values from -0.125 to 0.125
- log_rate: float32 [4], replicated, may hold values from 3 to 4
- copy_from: int32 [4], replicated, may hold values from 0 to 1, as said below
- perturb: int32 [4], replicated, may hold values from 0 to 2
Outputs:
- next_input: bfloat16 [4, 256, 2048], P('pop', 'dp')
- next_middle: bfloat16 [4, 2048, 2048], P('pop', 'dp')
- next_head: bfloat16 [4, 2048, 18], P('pop', 'dp')
- next_log_rate: float32 [4], P('pop')
- fitness: float32 [4], P('pop')
Inputs may be any that keep to these rules, and one draw needn't show every extreme that they name: Some two members that lie 4 apart have copy_from 1.
All inputs are finite; a program needn't handle non-finite values.
Results may differ from a plain program's by a relative error of at most 0.014.
Values may be sent and summed in bfloat16 or wider, within the bound.
No kernel may reach another device: no remote copies, remote signals or barrier semaphores. Data moves between devices by JAX's collectives and lax.ppermute only.
A program may use at most 128 MiB of HBM per device.

v0:
```python
import jax
import jax.numpy as jnp
from jax import lax
from jax.sharding import PartitionSpec as P

CAP = 2.0


def shifted(block, axis, distance):
    devices = range(lax.axis_size(axis))
    route = [((i - distance) % len(devices), i) for i in devices]
    return lax.ppermute(block, axis, route)


def silu_slope(pre):
    sig = jax.nn.sigmoid(pre)
    return sig * (1.0 + pre * (1.0 - sig))


def contract_rows(left, right):
    return lax.dot_general(
        left, right, (((0,), (0,)), ((), ())), preferred_element_type=jnp.float32
    )


def contract_cols(left, right):
    return lax.dot_general(
        left, right, (((1,), (1,)), ((), ())), preferred_element_type=jnp.float32
    )


def local(observations, returns, actions, w_input, w_middle, w_head, log_rate, copy_from, perturb):
    obs = observations[0]
    gains = returns[0]
    chosen = actions[0]
    own_first = w_input[0]
    own_middle = w_middle[0]
    own_head = w_head[0]
    rows = obs.shape[0]
    batch = rows * lax.axis_size("dp")
    first, head = (
        lax.all_gather(own_first, "dp", axis=0, tiled=True),
        lax.all_gather(own_head, "dp", axis=0, tiled=True),
    )
    pre1 = jnp.dot(obs, first, preferred_element_type=jnp.float32)
    hidden1 = jax.nn.silu(pre1).astype(jnp.bfloat16)
    columns = hidden1
    pre2 = jnp.dot(
        columns,
        lax.all_gather(own_middle, "dp", axis=0, tiled=True),
        preferred_element_type=jnp.float32,
    )
    hidden2 = jax.nn.silu(pre2).astype(jnp.bfloat16)
    squash = jnp.tanh(jnp.dot(hidden2, head, preferred_element_type=jnp.float32) / CAP)
    logits = CAP * squash
    logp = logits - jnp.log(jnp.sum(jnp.exp(logits), axis=1, keepdims=True))
    onehot = (chosen[:, None] == lax.broadcasted_iota(jnp.int32, logits.shape, 1)).astype(
        jnp.float32
    )
    taken = jnp.sum(logp * onehot, axis=1)
    fitness = lax.psum(jnp.sum(gains * taken) / batch, "dp")
    grad_raw = (
        -(gains / batch)[:, None] * (onehot - jnp.exp(logp)) * (1.0 - squash * squash)
    ).astype(jnp.bfloat16)
    head_term = contract_rows(hidden2, grad_raw)
    grad_pre2 = (contract_cols(grad_raw, head) * silu_slope(pre2)).astype(jnp.bfloat16)
    columns = hidden1
    grad_middle = lax.psum_scatter(
        contract_rows(columns, grad_pre2).astype(jnp.bfloat16),
        "dp",
        scatter_dimension=0,
        tiled=True,
    ).astype(jnp.float32)
    member = lax.axis_index("pop")
    members = lax.axis_size("pop")
    rate = jnp.exp(lax.dynamic_index_in_dim(log_rate, member, keepdims=False))
    new_middle = (own_middle.astype(jnp.float32) - rate * grad_middle).astype(jnp.bfloat16)
    back = contract_cols(grad_pre2, lax.all_gather(own_middle, "dp", axis=0, tiled=True))
    grad_pre1 = (back * silu_slope(pre1)).astype(jnp.bfloat16)
    input_term = contract_rows(obs, grad_pre1)
    grad_first, grad_head = (
        lax.psum_scatter(
            input_term.astype(jnp.bfloat16), "dp", scatter_dimension=0, tiled=True
        ).astype(jnp.float32),
        lax.psum_scatter(
            head_term.astype(jnp.bfloat16), "dp", scatter_dimension=0, tiled=True
        ).astype(jnp.float32),
    )
    new_first = (own_first.astype(jnp.float32) - rate * grad_first).astype(jnp.bfloat16)
    new_head = (own_head.astype(jnp.float32) - rate * grad_head).astype(jnp.bfloat16)
    moved_first, moved_middle, moved_head = shifted((new_first, new_middle, new_head), "pop", 1)
    flag = lax.dynamic_index_in_dim(copy_from, member, keepdims=False) == 1
    out_first = jnp.where(flag, moved_first, new_first)
    out_middle = jnp.where(flag, moved_middle, new_middle)
    out_head = jnp.where(flag, moved_head, new_head)
    source = jnp.where(flag, (member + members - 1) % members, member)
    pick = lax.dynamic_index_in_dim(perturb, member, keepdims=False)
    offset = jnp.where(pick == 0, -0.2, jnp.where(pick == 1, 0.0, 0.2)).astype(jnp.float32)
    next_rate = lax.dynamic_index_in_dim(log_rate, source, keepdims=False) + offset
    return (
        out_first[None],
        out_middle[None],
        out_head[None],
        next_rate.reshape(1),
        fitness.reshape(1),
    )


def solution(mesh):
    in_specs = (
        P("pop", "dp", None),
        P("pop", "dp"),
        P("pop", "dp"),
        P("pop", "dp", None),
        P("pop", "dp", None),
        P("pop", "dp", None),
        P(),
        P(),
        P(),
    )
    out_specs = (
        P("pop", "dp", None),
        P("pop", "dp", None),
        P("pop", "dp", None),
        P("pop"),
        P("pop"),
    )
    return jax.shard_map(local, mesh=mesh, in_specs=in_specs, out_specs=out_specs, check_vma=False)
```

profile of v0, /device:TPU:0, one launch (start us, length us, event | category | flops | bytes accessed | tf_op | source)
XLA Modules:
  0.0 336.1 jit_solution(15053843083889888465)
XLA Ops:
  8.0 0.7 all-gather.8.cloned.1.call-update
  8.7 16.0 %all-gather.2 = bf16[1,2048,18]{1,2,0:T(8,128)(2,1)S(1)} all-gather(bf16[1,256,18]{1,2,0:T(8,128)(2,1)} %param.14), channel_id=4, replica_groups=mesh['pop'=4,'dp'=8] {'dp'}, dimensions={1}, use_global_device_ids=true | all-gather | bytes 82944 | tf_op jit(solution)/shard_map/all_gather | solution.py:43
  24.7 9.9 %all-gather.6.cloned.1.call-done = bf16[1,256,2048]{2,1,0:T(8,128)(2,1)} async-done(((bf16[1,32,2048]{2,1,0:T(8,128)(2,1)}), bf16[1,256,2048]{2,1,0:T(8,128)(2,1)}) %all-gather.6.cloned.1.call-update) | async-done | bytes 1048592 | tf_op jit(solution)/shard_map/all_gather | solution.py:42
  34.6 3.9 %fusion.19 = f32[512,2048]{1,0:T(8,128)} fusion(bf16[1,256,2048]{2,1,0:T(8,128)(2,1)} %all-gather.6.cloned.1.call-done, bf16[1,512,256]{2,1,0:T(8,128)(2,1)S(1)} %copy-done), kind=kOutput, calls=%fused_computation.22 | convolution fusion | flops 536870912 | bytes 5505024 | tf_op jit(solution)/shard_map/dot_general | solution.py:45
  38.5 79.6 %all-gather.8.cloned.1.call-done = bf16[1,2048,2048]{2,1,0:T(8,128)(2,1)} async-done(((bf16[1,256,2048]{2,1,0:T(8,128)(2,1)}), bf16[1,2048,2048]{2,1,0:T(8,128)(2,1)}) %all-gather.8.cloned.1.call-update) | async-done | bytes 8388624 | tf_op jit(solution)/shard_map/all_gather | solution.py:50
  118.1 11.5 %multiply_convert_fusion.2 = (bf16[512,2048]{1,0:T(8,128)(2,1)S(1)}, f32[512,2048]{1,0:T(8,128)}) fusion(bf16[1,2048,2048]{2,1,0:T(8,128)(2,1)} %all-gather.8.cloned.1.call-done, f32[512,2048]{1,0:T(8,128)} %fusion.19), kind=kOutput, calls=%fused_computation.7 | convolution fusion | flops 4305453056 | bytes 18874368 | tf_op jit(solution)/shard_map/dot_general | solution.py:48
  131.0 1.0 convolution_convert_fusion.1
  132.0 3.9 %multiply_convert_fusion.1 = bf16[512,2048]{1,0:T(8,128)(2,1)S(1)} fusion(f32[512,2048]{1,0:T(8,128)} %get-tuple-element.20, bf16[1,2048,18]{1,2,0:T(8,128)(2,1)S(1)} %all-gather.2, f32[512,18]{0,1:T(8,128)S(1)} %get-tuple-element.22, f32[512]{0:T(512)S(1)} %log.8, s32[512]{0:T(512)S(1)} %bitcast.59, f32[512]{0:T(512)S(1)} %get-tuple-element.16), kind=kOutput, calls=%fused_computation.6 | convolution fusion | flops 47278080 | bytes 6408192 | tf_op jit(solution)/shard_map/dot_general | solution.py:27
  135.9 9.0 %fusion.12 = bf16[256,2048]{0,1:T(8,128)(2,1)S(1)} fusion(f32[512,2048]{1,0:T(8,128)} %fusion.19, bf16[512,2048]{1,0:T(8,128)(2,1)S(1)} %multiply_convert_fusion.1, bf16[1,2048,2048]{2,1,0:T(8,128)(2,1)} %all-gather.8.cloned.1.call-done, bf16[1,512,256]{2,1,0:T(8,128)(2,1)S(1)} %copy-done), kind=kOutput, calls=%fused_computation.13 | convolution fusion | flops 4841799680 | bytes 15990784 | tf_op jit(solution)/shard_map/dot_general | solution.py:21
  144.9 1.4 copy.18
  146.6 9.2 %convolution_convert_fusion = bf16[2048,2048]{1,0:T(8,128)(2,1)} fusion(bf16[512,2048]{1,0:T(8,128)(2,1)S(1)} %multiply_convert_fusion.1, f32[512,2048]{1,0:T(8,128)} %fusion.19), kind=kOutput, calls=%fused_computation.4 | convolution fusion | flops 4304404480 | bytes 14680064 | tf_op jit(solution)/shard_map/dot_general | solution.py:21
  155.8 0.8 copy-done.2
  162.9 15.2 %psum.7 = f32[1]{0:T(128)} all-reduce(f32[1]{0:T(128)} %bitcast.15), channel_id=1, replica_groups=mesh['pop'=4,'dp'=8] {'dp'}, use_global_device_ids=true, to_apply=%region_6.7 | all-reduce | flops 1 | bytes 8 | tf_op jit(solution)/shard_map/psum | solution.py:61
  178.1 0.7 fusion.25
  178.8 1.7 collective-permute-start.2
  180.5 18.0 %reduce-scatter.10.cloned.1.call-done = bf16[32,2048]{1,0:T(8,128)(2,1)} async-done(((bf16[256,2048]{1,0:T(8,128)(2,1)}), bf16[32,2048]{1,0:T(8,128)(2,1)}) %reduce-scatter.10.cloned.1.call-update) | async-done | bytes 131088
  198.5 1.2 copy.19
  199.7 88.7 %reduce-scatter.6.cloned.1.call-done = bf16[256,2048]{1,0:T(8,128)(2,1)} async-done(((bf16[2048,2048]{1,0:T(8,128)(2,1)}), bf16[256,2048]{1,0:T(8,128)(2,1)}) %reduce-scatter.6.cloned.1.call-update) | async-done | bytes 1048592 | tf_op jit(solution)/shard_map/reduce_scatter | solution.py:68
  288.4 1.6 fusion.15
  290.1 1.5 collective-permute-start.1
  291.7 1.5 collective-permute-start
  293.9 31.4 %collective-permute-done = bf16[32,2048]{0,1:T(8,128)(2,1)S(1)} collective-permute-done((bf16[32,2048]{0,1:T(8,128)(2,1)S(1)}, bf16[32,2048]{0,1:T(8,128)(2,1)S(1)}, u32[]{:S(2)}, u32[]{:S(2)}) %collective-permute-start) | collective-permute-done | bytes 131104 | tf_op jit(solution)/shard_map/ppermute | solution.py:12
  325.3 0.8 copy.17
  326.2 2.3 select_bitcast_fusion
  (40 shorter events, 5.4 us)
Async XLA Ops:
  7.2 27.4 %copy-start = (bf16[1,512,256]{2,1,0:T(8,128)(2,1)S(1)}, bf16[1,512,256]{2,1,0:T(8,128)(2,1)}, u32[]{:S(2)}) copy-start(bf16[1,512,256]{2,1,0:T(8,128)(2,1)} %param.9) | copy-start | bytes 786436
  7.2 27.4 %all-gather.6.cloned.1.call-start = ((), (), s32[]{:S(2)}) async-start(), calls=%async_computation.5 | async-start | bytes 1179648 | tf_op jit(solution)/shard_map/all_gather | solution.py:42
  7.9 110.2 %all-gather.8.cloned.1.call-start = ((), (), s32[]{:S(2)}) async-start(), calls=%async_computation.6 | async-start | bytes 9437184 | tf_op jit(solution)/shard_map/all_gather | solution.py:50
  8.7 169.4 %reduce-scatter.8.cloned.1.call-start = ((), (), s32[]{:S(2)}) async-start(), calls=%async_computation.4 | async-start | bytes 110592 | tf_op jit(solution)/shard_map/reduce_scatter | solution.py:85
  38.5 91.8 %copy-start.4 = (s32[1,512]{1,0:T(1,128)S(1)}, s32[1,512]{1,0:T(1,128)}, u32[]{:S(2)}) copy-start(s32[1,512]{1,0:T(1,128)} %param.11) | copy-start | bytes 6148
  38.5 91.9 %copy-start.6 = (f32[1,512]{1,0:T(1,128)S(1)}, f32[1,512]{1,0:T(1,128)}, u32[]{:S(2)}) copy-start(f32[1,512]{1,0:T(1,128)} %param.10) | copy-start | bytes 6148
  135.9 62.7 %reduce-scatter.10.cloned.1.call-start = ((), (), s32[]{:S(2)}) async-start(), calls=%async_computation.7 | async-start | bytes 1179648
  146.4 142.1 %reduce-scatter.6.cloned.1.call-start = ((), (), s32[]{:S(2)}) async-start(), calls=%async_computation.3 | async-start | bytes 9437184 | tf_op jit(solution)/shard_map/reduce_scatter | solution.py:68
  155.8 0.9 copy-start.2
  155.8 1.2 copy-start.7
  155.8 2.5 copy-start.5
  155.8 3.8 %copy-start.8 = (s32[4]{0:T(128)S(1)}, s32[4]{0:T(128)}, u32[]{:S(2)}) copy-start(s32[4]{0:T(128)} %param.17) | copy-start | bytes 52
  155.8 22.3 %copy-start.3 = (bf16[1,256,18]{1,2,0:T(8,128)(2,1)S(1)}, bf16[1,256,18]{1,2,0:T(8,128)(2,1)}, u32[]{:S(2)}) copy-start(bf16[1,256,18]{1,2,0:T(8,128)(2,1)} %param.14) | copy-start | bytes 27652
  155.8 132.6 %copy-start.1 = (bf16[1,256,2048]{2,1,0:T(8,128)(2,1)S(1)}, bf16[1,256,2048]{2,1,0:T(8,128)(2,1)}, u32[]{:S(2)}) copy-start(bf16[1,256,2048]{2,1,0:T(8,128)(2,1)} %param.13) | copy-start | bytes 3145732
  178.8 114.5 %collective-permute-start.2 = (bf16[256,18]{0,1:T(8,128)(2,1)S(1)}, bf16[256,18]{0,1:T(8,128)(2,1)S(1)}, u32[]{:S(2)}, u32[]{:S(2)}) collective-permute-start(bf16[256,18]{0,1:T(8,128)(2,1)S(1)} %fusion.25), channel_id=1, source_target_pairs={{24,0},{0,8},{8,16},{16,24},{25,1},{1,9},{9,17},{17,25},{26,2},{2,... | collective-permute-start | bytes 27656 | tf_op jit(solution)/shard_map/ppermute | solution.py:12
  290.1 36.1 %collective-permute-start.1 = (bf16[256,2048]{1,0:T(8,128)(2,1)S(1)}, bf16[256,2048]{1,0:T(8,128)(2,1)}, u32[]{:S(2)}, u32[]{:S(2)}) collective-permute-start(bf16[256,2048]{1,0:T(8,128)(2,1)S(1)} %fusion.15), channel_id=1, source_target_pairs={{24,0},{0,8},{8,16},{16,24},{25,1},{1,9},{9,17},{17,25},{26,2},{2,... | collective-permute-start | bytes 3145736 | tf_op jit(solution)/shard_map/ppermute | solution.py:12
  291.7 33.5 %collective-permute-start = (bf16[32,2048]{0,1:T(8,128)(2,1)S(1)}, bf16[32,2048]{0,1:T(8,128)(2,1)S(1)}, u32[]{:S(2)}, u32[]{:S(2)}) collective-permute-start(bf16[32,2048]{0,1:T(8,128)(2,1)S(1)} %fusion.18), channel_id=1, source_target_pairs={{24,0},{0,8},{8,16},{16,24},{25,1},{1,9},{9,17},{17,25},{26,2},{2,... | collective-permute-start | bytes 393224 | tf_op jit(solution)/shard_map/ppermute | solution.py:12
Sparse Core Ops, SparseCore 0:
  9.6 24.9 all-gather.5
  36.2 81.8 all-gather.7
  136.0 29.0 reduce-scatter.7
  167.8 30.7 reduce-scatter.9
  200.7 87.6 reduce-scatter.5
where the time goes:
time: 337 us; the launch traced here: 336 us
  waiting for transfers between devices  229 us (68%)
  matrix products  39.2 us (12%)
  blocking collectives  31.2 us (9%)
  between operations  19.1 us (6%)
  local copies, waits for them, and re-layouts  6.44 us (2%)
  other arithmetic  6.09 us (2%)
  starting transfers between devices  5.14 us (2%)
    reduce_scatter x1, waiting for transfers between devices, local(): lax.psum_scatter(contract_rows(columns, grad_pre2).astype(jnp.bfloat16),...  88.7 us
    all_gather x1, waiting for transfers between devices, local(): lax.all_gather(own_middle, 'dp', axis=0, tiled=True)  79.6 us
    ppermute x3, waiting for transfers between devices, shifted(): return lax.ppermute(block, axis, route)  31.4 us
    unnamed x6, waiting for transfers between devices  19.4 us
    dot_general x3, matrix products, contract_rows(): lax.dot_general(left, right, (((0,), (0,)), ((), ())), preferred_element_...  19.2 us
    all_gather x1, blocking collectives, local(): lax.all_gather(own_head, 'dp', axis=0, tiled=True)  16 us
    psum x1, blocking collectives, local(): fitness = lax.psum(jnp.sum(gains * taken) / batch, 'dp')  15.2 us
    dot_general x1, matrix products, local(): jnp.dot(columns, lax.all_gather(own_middle, 'dp', axis=0, tiled=True), pr...  11.5 us
  transfers between devices with their start and end apart: 8, of which 5 were waited for; matrix products, arithmetic and copies ran while one was open for 9% of the time, Pallas kernels for 0%

commit v1 on v0

--- a/solution.py
+++ b/solution.py
@@ -1,32 +1,660 @@
 import jax
 import jax.numpy as jnp
 from jax import lax
+from jax.experimental import pallas as pl
+from jax.experimental.pallas import tpu as pltpu
 from jax.sharding import PartitionSpec as P
 
 CAP = 2.0
+CHUNKS = 4
+GROUPS = 2
+
+
+def silu_slope(pre):
+    sig = jax.nn.sigmoid(pre)
+    return sig * (1.0 + pre * (1.0 - sig))
+
+
+def contract_rows(left, right):
+    return lax.dot_general(
+        left, right, (((0,), (0,)), ((), ())), preferred_element_type=jnp.float32
+    )
+
+
+def contract_cols(left, right):
+    return lax.dot_general(
+        left, right, (((1,), (1,)), ((), ())), preferred_element_type=jnp.float32
+    )
+
+
+def sigmoid(v):
+    return 0.5 + 0.5 * jnp.tanh(0.5 * v)
+
+
+def dot(left, right, dims=((1,), (0,))):
+    return lax.dot_general(left, right, (dims, ((), ())), preferred_element_type=jnp.float32)
+
+
+def params(mib, *semantics):
+    return pltpu.CompilerParams(dimension_semantics=semantics or None, vmem_limit_bytes=mib << 20)
+
+
+def hbm(array):
+    return pltpu.with_memory_space_constraint(array, pltpu.HBM)
+
+
+def whole(array):
+    return pl.BlockSpec(array.shape, lambda *_: (0,) * array.ndim)
+
+
+def cost(flops, moved):
+    return pl.CostEstimate(flops=int(flops), bytes_accessed=int(moved), transcendentals=0)
+
+
+def first_layer(order, pieces, theirs, rows, slab, near_blocks):
+    count = len(pieces)
+    devices = 2 * count
+    features = pieces[0].shape[1]
+    each = features // devices
+    mids = devices * each
+    pad_acts = pieces[0].shape[0] - rows - mids
+    width = devices * slab
+    total = count * rows
+    near_all = 2 * near_blocks
+
+    def near_at(i):
+        return (i // count) * near_blocks + jnp.minimum(i % count, near_blocks - 1)
+
+    def kernel(order_ref, *refs):
+        piece_refs, theirs_ref = refs[:count], refs[count]
+        h1_ref, h1t_ref, slope_ref, obst_ref, head_ref, cols = refs[count + 1 :]
+        i = pl.program_id(0)
+
+        def small(k, start, size):
+            if k < count:
+                return piece_refs[k][pl.ds(rows + start, size), :]
+            return theirs_ref[k - count, pl.ds(start, size), :]
+
+        @pl.when(i == 0)
+        def _():
+            for k in range(devices):
+                at = pl.multiple_of(order_ref[k] * each, each)
+                lanes = pl.multiple_of(order_ref[k] * slab, slab)
+                head_ref[:, pl.ds(lanes, slab)] = small(k, mids, pad_acts)
+                for b in range(devices):
+                    source = pl.multiple_of(order_ref[b] * each, each)
+                    cols[b, pl.ds(at, each), :] = small(k, source, each)
+            for p in range(count):
+                block = piece_refs[p][:rows, :].astype(jnp.float32)
+                obst_ref[:, p * rows : (p + 1) * rows] = block.T.astype(jnp.bfloat16)
+
+        weights = cols[i]
+        for p in range(count):
+            pre = dot(piece_refs[p][:rows, :], weights)
+            h1_ref[p * rows : (p + 1) * rows, :] = (pre * sigmoid(pre)).astype(jnp.bfloat16)
+
+        @pl.when(i % count < near_blocks)
+        def _():
+            for p in range(count):
+                obs = piece_refs[p][:rows, :]
+                pre = dot(obs, weights)
+                sig = sigmoid(pre)
+                slope_ref[p * rows : (p + 1) * rows, :] = (sig * (1.0 + pre * (1.0 - sig))).astype(jnp.bfloat16)
+                pre_t = dot(weights, obs, ((0,), (1,)))
+                h1t_ref[:, p * rows : (p + 1) * rows] = (pre_t * sigmoid(pre_t)).astype(jnp.bfloat16)
+
+    shape = lambda *s: jax.ShapeDtypeStruct(s, jnp.bfloat16)
+    return pl.pallas_call(
+        kernel,
+        name="first_layer",
+        grid_spec=pltpu.PrefetchScalarGridSpec(
+            num_scalar_prefetch=1,
+            grid=(devices,),
+            in_specs=[whole(p) for p in pieces] + [whole(theirs)],
+            out_specs=[
+                pl.BlockSpec((total, slab), lambda i, _: (0, i)),
+                pl.BlockSpec((slab, total), lambda i, _: (near_at(i), 0)),
+                pl.BlockSpec((total, slab), lambda i, _: (0, near_at(i))),
+                pl.BlockSpec((features, total), lambda i, _: (0, 0)),
+                pl.BlockSpec((pad_acts, width), lambda i, _: (0, 0)),
+            ],
+            scratch_shapes=[pltpu.VMEM((devices, features, slab), jnp.bfloat16)],
+        ),
+        out_shape=[
+            shape(total, width),
+            shape(near_all * slab, total),
+            pltpu.HBM((total, near_all * slab), jnp.bfloat16),
+            pltpu.HBM((features, total), jnp.bfloat16),
+            shape(pad_acts, width),
+        ],
+        cost_estimate=cost(2 * total * features * width * 2, 30 << 20),
+        compiler_params=params(20, "arbitrary"),
+    )(order, *map(hbm, pieces), hbm(theirs))
+
+
+def second_layer(hidden1, own, pieces, theirs, head, logits, hidden2, q, cut):
+    total, width = hidden1.shape
+    slab = own.shape[0]
+    pad_acts = head.shape[0]
+    tile = min(512, total)
+    first = logits is None
+    sub = 256
+
+    def kernel(h1_ref, own_ref, *refs):
+        piece_refs = refs[: len(pieces)]
+        theirs_ref, head_ref = refs[len(pieces) : len(pieces) + 2]
+        rest = refs[len(pieces) + 2 :]
+        logits_in = None if first else rest[0]
+        h2_ref, slope_ref, logits_ref, weights = rest[0 if first else 2 :]
+
+        @pl.when(pl.program_id(0) == 0)
+        def _():
+            weights[:slab] = own_ref[...]
+            for k, piece in enumerate(piece_refs):
+                weights[(k + 1) * slab : (k + 2) * slab] = piece[...]
+            weights[(len(pieces) + 1) * slab :] = theirs_ref[...]
+
+        for r in range(0, tile, sub):
+            pre = dot(h1_ref[r : r + sub, :], weights[...])
+            sig = sigmoid(pre)
+            hidden = (pre * sig).astype(jnp.bfloat16)
+            h2_ref[r : r + sub, :] = hidden
+            slope_ref[r : r + sub, :] = (sig * (1.0 + pre * (1.0 - sig))).astype(jnp.bfloat16)
+            part = dot(hidden, head_ref[...], ((1,), (1,)))
+            logits_ref[r : r + sub, :] = part if first else part + logits_in[r : r + sub, :]
+
+    row = lambda size: pl.BlockSpec((tile, size), lambda i: (i, 0))
+    return pl.pallas_call(
+        kernel,
+        name="second_layer",
+        grid=(total // tile,),
+        in_specs=[row(width), pl.BlockSpec((slab, cut), lambda i: (0, q))]
+        + [whole(p) for p in pieces]
+        + [whole(theirs), pl.BlockSpec((pad_acts, cut), lambda i: (0, q))]
+        + ([] if first else [row(pad_acts), pl.BlockSpec(memory_space=pltpu.HBM)]),
+        out_specs=[pl.BlockSpec((tile, cut), lambda i: (i, q)), row(cut), row(pad_acts)],
+        out_shape=[
+            pltpu.HBM((total, width), jnp.bfloat16),
+            jax.ShapeDtypeStruct((total, cut), jnp.bfloat16),
+            jax.ShapeDtypeStruct((total, pad_acts), jnp.float32),
+        ],
+        scratch_shapes=[pltpu.VMEM((width, cut), jnp.bfloat16)],
+        input_output_aliases={} if first else {len(pieces) + 5: 0},
+        cost_estimate=cost(2 * total * width * cut, 16 << 20),
+        compiler_params=params(18, "arbitrary"),
+    )(hidden1, hbm(own), *map(hbm, pieces), hbm(theirs), head, *([] if first else [logits, hbm(hidden2)]))
+
+
+def policy(logits_raw, labels, acts, batch):
+    total, pad_acts = logits_raw.shape
+
+    def kernel(raw_ref, labels_ref, graw_ref, graw_t_ref, score_ref):
+        raw = raw_ref[...].T
+        gains, chosen = labels_ref[0:1, :], labels_ref[1:2, :].astype(jnp.int32)
+        at = lax.broadcasted_iota(jnp.int32, raw.shape, 0)
+        live = at < acts
+        squash = jnp.tanh(raw / CAP)
+        logits = CAP * squash
+        mass = jnp.sum(jnp.where(live, jnp.exp(logits), 0.0), axis=0, keepdims=True)
+        logp = logits - jnp.log(mass)
+        onehot = at == chosen
+        taken = jnp.sum(jnp.where(onehot, logp, 0.0), axis=0, keepdims=True)
+        score_ref[...] = jnp.sum(gains * taken, axis=1, keepdims=True) / batch
+        grad = -(gains / batch) * (onehot.astype(jnp.float32) - jnp.exp(logp)) * (1.0 - squash * squash)
+        grad = jnp.where(live, grad, 0.0)
+        graw_t_ref[...] = grad.astype(jnp.bfloat16)
+        graw_ref[...] = grad.T.astype(jnp.bfloat16)
+
+    return pl.pallas_call(
+        kernel,
+        name="policy",
+        out_shape=[
+            jax.ShapeDtypeStruct((total, pad_acts), jnp.bfloat16),
+            jax.ShapeDtypeStruct((pad_acts, total), jnp.bfloat16),
+            jax.ShapeDtypeStruct((1, 1), jnp.float32),
+        ],
+        cost_estimate=cost(1 << 28, 2 << 20),
+        compiler_params=params(10),
+    )(logits_raw, labels)
+
+
+def middle_grad(graw, head, slopes, hidden1_t, first, cut):
+    total, pad_acts = graw.shape
+    near_rows = hidden1_t.shape[0]
+    kept = near_rows // 2
+    tile = min(256, kept)
+    steps = near_rows // tile
+    parts = len(slopes)
+    span = parts * cut
+
+    def kernel(graw_ref, head_ref, *refs):
+        slope_refs = refs[:parts]
+        h1t_ref, g2_ref, keep_ref, give_ref = refs[parts:]
+        i = pl.program_id(0)
+
+        @pl.when(i == 0)
+        def _():
+            for p in range(parts):
+                lanes = slice(p * cut, (p + 1) * cut)
+                for r in range(0, total, 256):
+                    g2 = dot(graw_ref[r : r + 256, :], head_ref[:, lanes]) * slope_refs[p][r : r + 256, :].astype(jnp.float32)
+                    g2_ref[r : r + 256, lanes] = g2.astype(jnp.bfloat16)
+
+        part = dot(h1t_ref[...], g2_ref[...])
+
+        @pl.when(i < steps // 2)
+        def _():
+            give_ref[...] = part.astype(jnp.bfloat16)
+
+        @pl.when(i >= steps // 2)
+        def _():
+            keep_ref[...] = part
+
+    turn = lambda i: (i + steps // 2) % steps
+    return pl.pallas_call(
+        kernel,
+        name="middle_grad",
+        grid=(steps,),
+        in_specs=[whole(graw), pl.BlockSpec((pad_acts, span), lambda i: (0, first // parts))]
+        + [whole(v) for v in slopes]
+        + [pl.BlockSpec((tile, total), lambda i: (turn(i), 0))],
+        out_specs=[
+            pl.BlockSpec((total, span), lambda i: (0, 0)),
+            pl.BlockSpec((tile, span), lambda i: (jnp.maximum(i - steps // 2, 0), 0)),
+            pl.BlockSpec((tile, span), lambda i: (jnp.minimum(i, steps // 2 - 1), 0)),
+        ],
+        out_shape=[
+            jax.ShapeDtypeStruct((total, span), jnp.bfloat16),
+            jax.ShapeDtypeStruct((kept, span), jnp.float32),
+            pltpu.HBM((kept, span), jnp.bfloat16),
+        ],
+        cost_estimate=cost(2 * total * near_rows * span, 16 << 20),
+        compiler_params=params(24, "arbitrary"),
+    )(graw, head, *slopes, hidden1_t)
+
+
+def head_grad(scalars, graw_t, hidden2):
+    pad_acts, total = graw_t.shape
+    side = hidden2.shape[1] // 2
+    block = min(512, side)
+
+    def kernel(scalar_ref, graw_t_ref, h2_ref, out_ref):
+        out_ref[...] = dot(graw_t_ref[...], h2_ref[...])
+
+    return pl.pallas_call(
+        kernel,
+        name="head_grad",
+        grid_spec=pltpu.PrefetchScalarGridSpec(
+            num_scalar_prefetch=1,
+            grid=(side // block,),
+            in_specs=[
+                pl.BlockSpec((pad_acts, total), lambda i, _: (0, 0)),
+                pl.BlockSpec((total, block), lambda i, s: (0, s[1] * (side // block) + i)),
+            ],
+            out_specs=pl.BlockSpec((pad_acts, block), lambda i, _: (0, i)),
+        ),
+        out_shape=jax.ShapeDtypeStruct((pad_acts, side), jnp.float32),
+        cost_estimate=cost(2 * total * side * 256, 6 << 20),
+        compiler_params=params(10, "arbitrary"),
+    )(scalars, graw_t, hbm(hidden2))
+
+
+def middle_update(rate, keep, got, own, near_pieces, group, span, cut):
+    slab = own.shape[0]
+    per = span // cut
+    blocks = 1 + len(near_pieces[0])
+    flat = [p for chunk in near_pieces for p in chunk]
+
+    def kernel(rate_ref, keep_ref, got_ref, own_ref, *refs):
+        flat_refs, out_refs = refs[: len(flat)], refs[len(flat) :]
+        rate = rate_ref[0:1, 0:1]
+        for s in reversed(range(blocks)):
+            for p in range(per):
+                lanes, at = slice(p * cut, (p + 1) * cut), slice(s * slab, (s + 1) * slab)
+                weight = own_ref[:, lanes] if s == 0 else flat_refs[p * (blocks - 1) + s - 1][...]
+                total = keep_ref[at, lanes] + got_ref[at, lanes].astype(jnp.float32)
+                out_refs[s][:, lanes] = (weight.astype(jnp.float32) - rate * total).astype(jnp.bfloat16)
+
+    return pl.pallas_call(
+        kernel,
+        name="middle_update",
+        grid=(1,),
+        in_specs=[whole(rate), whole(keep), whole(got)]
+        + [pl.BlockSpec((slab, span), lambda i: (0, group))]
+        + [whole(p) for p in flat],
+        out_specs=[pl.BlockSpec((slab, span), lambda i: (0, 0))] * blocks,
+        out_shape=[pltpu.HBM((slab, span), jnp.bfloat16)] * blocks,
+        cost_estimate=cost(1 << 27, 4 << 20),
+        compiler_params=params(16, "arbitrary"),
+    )(rate, keep, hbm(got), hbm(own), *map(hbm, flat))
+
+
+def gather_small(scalars, order, keep, got, side, score, first_rows, slab, half):
+    count = 2 * half
+    devices = 2 * count
+    mids = devices * first_rows
+    pad_acts = side.shape[0]
+    acts_at = mids + pad_acts
+
+    def kernel(scalar_ref, order_ref, keep_ref, got_ref, side_ref, score_ref, mine_ref, sent_ref):
+        core = scalar_ref[0]
+        for target, which in ((sent_ref, 1 - core), (mine_ref, core)):
+            for j in range(half):
+                base = pl.multiple_of(j * 2 * first_rows + which * first_rows, first_rows)
+                for k in range(devices):
+                    source = got_ref if (k // half) % 2 else keep_ref
+                    lanes = ((k // count) * half + k % half) * slab
+                    at = pl.multiple_of(order_ref[k] * first_rows, first_rows)
+                    target[j, pl.ds(at, first_rows), :] = source[pl.ds(base, first_rows), lanes : lanes + slab]
+                cols = pl.multiple_of((j * 2 + which) * slab, slab)
+                target[j, mids:acts_at, :] = side_ref[:, pl.ds(cols, slab)].astype(jnp.bfloat16)
+        value = jnp.broadcast_to(score_ref[...], (1, slab))
+        for part in range(3):
+            piece = value.astype(jnp.bfloat16)
+            sent_ref[0, acts_at - 3 + part : acts_at - 2 + part, :] = piece
+            value = value - piece.astype(jnp.float32)
+
+    shape = jax.ShapeDtypeStruct((half, acts_at, slab), jnp.bfloat16)
+    smem = pl.BlockSpec(memory_space=pltpu.SMEM)
+    arrays = [keep, hbm(got), side, score]
+    return pl.pallas_call(
+        kernel,
+        name="gather_small",
+        grid=(1,),
+        in_specs=[smem, smem] + [whole(v) for v in arrays],
+        out_specs=[whole(shape)] * 2,
+        out_shape=[shape, pltpu.HBM(shape.shape, shape.dtype)],
+        cost_estimate=cost(1 << 26, 2 << 20),
+        compiler_params=params(8, "arbitrary"),
+    )(scalars, order, *arrays)
+
+
+def small_update(scalars, rate, mine, got, weights, score):
+    half, rows, slab = mine.shape
+
+    def kernel(scalar_ref, rate_ref, mine_ref, got_ref, *refs):
+        weight_refs = refs[:half]
+        score_ref, fitness_ref = refs[half], refs[half + 1]
+        out_refs = refs[half + 2 :]
+        rate, high = rate_ref[0:1, 0:1], scalar_ref[1]
+        fitness = jnp.broadcast_to(score_ref[...], (1, slab))
+        for part in range(3):
+            fitness = fitness + got_ref[0, rows - 3 + part : rows - 2 + part, :].astype(jnp.float32)
+        fitness_ref[...] = fitness[:, :1]
+        for s in range(half):
+            at = jnp.where(high == 1, s, half - 1 - s)
+            total = mine_ref[at].astype(jnp.float32) + got_ref[at].astype(jnp.float32)
+            out_refs[s][...] = (weight_refs[s][-rows:, :].astype(jnp.float32) - rate * total).astype(jnp.bfloat16)
+            value = fitness
+            for part in range(3):
+                piece = value.astype(jnp.bfloat16)
+                out_refs[s][rows - 3 + part : rows - 2 + part, :] = piece
+                value = value - piece.astype(jnp.float32)
+
+    smem = pl.BlockSpec(memory_space=pltpu.SMEM)
+    return pl.pallas_call(
+        kernel,
+        name="small_update",
+        grid=(1,),
+        in_specs=[smem] + [whole(v) for v in (rate, mine, got, *weights, score)],
+        out_specs=[pl.BlockSpec((1, 1), lambda i: (0, 0))] + [pl.BlockSpec((rows, slab), lambda i: (0, 0))] * half,
+        out_shape=[jax.ShapeDtypeStruct((1, 1), jnp.float32)] + [pltpu.HBM((rows, slab), jnp.bfloat16)] * half,
+        cost_estimate=cost(1 << 26, 2 << 20),
+        compiler_params=params(8, "arbitrary"),
+    )(scalars, rate, mine, hbm(got), *map(hbm, weights), score)
+
+
+def input_grad(scalars, grads, own, near_pieces, theirs, slope, obs_t, cut):
+    total = grads[0].shape[0]
+    slab, width = own.shape
+    near_rows = slope.shape[1]
+    kept = near_rows // 2
+    features = obs_t.shape[0]
+    groups = len(grads)
+    chunks = len(theirs)
+    side = features // 2
+    tile = min(256, total)
+    flat = [p for chunk in near_pieces for p in chunk]
+    per = len(flat) // chunks
+
+    def kernel(scalar_ref, *refs):
+        g_refs, refs = refs[:groups], refs[groups:]
+        own_ref, refs = refs[0], refs[1:]
+        flat_refs, refs = refs[: len(flat)], refs[len(flat) :]
+        theirs_refs, refs = refs[:chunks], refs[chunks:]
+        slope_ref, obst_ref, keep_ref, give_ref, weights, total_ref = refs
+        i = pl.program_id(0)
+
+        @pl.when(i == 0)
+        def _():
+            weights[:slab] = own_ref[...]
+            for q in range(chunks):
+                lanes = slice(q * cut, (q + 1) * cut)
+                for k in range(per):
+                    weights[(k + 1) * slab : (k + 2) * slab, lanes] = flat_refs[q * per + k][...]
+                weights[kept:, lanes] = theirs_refs[q][...]
+            total_ref[...] = jnp.zeros_like(total_ref)
+
+        g2 = jnp.concatenate([g[...] for g in g_refs], axis=1)
+        back = dot(g2, weights[...], ((1,), (1,)))
+        grad = (back * slope_ref[...].astype(jnp.float32)).astype(jnp.bfloat16)
+        total_ref[...] += dot(obst_ref[...], grad)
+
+        @pl.when(i == pl.num_programs(0) - 1)
+        def _():
+            high = scalar_ref[1]
+            keep_ref[...] = total_ref[pl.ds(pl.multiple_of(high * side, side), side), :].astype(jnp.bfloat16)
+            give_ref[...] = total_ref[pl.ds(pl.multiple_of((1 - high) * side, side), side), :].astype(jnp.bfloat16)
+
+    return pl.pallas_call(
+        kernel,
+        name="input_grad",
+        grid=(total // tile,),
+        in_specs=[pl.BlockSpec(memory_space=pltpu.SMEM)]
+        + [pl.BlockSpec((tile, g.shape[1]), lambda i: (i, 0)) for g in grads]
+        + [whole(own)]
+        + [whole(p) for p in flat]
+        + [pl.BlockSpec((kept, cut), lambda i: (0, 0))] * chunks
+        + [pl.BlockSpec((tile, near_rows), lambda i: (i, 0)), pl.BlockSpec((features, tile), lambda i: (0, i))],
+        out_specs=[pl.BlockSpec((side, near_rows), lambda i: (0, 0))] * 2,
+        out_shape=[
+            jax.ShapeDtypeStruct((side, near_rows), jnp.bfloat16),
+            pltpu.HBM((side, near_rows), jnp.bfloat16),
+        ],
+        scratch_shapes=[
+            pltpu.VMEM((near_rows, width), jnp.bfloat16),
+            pltpu.VMEM((features, near_rows), jnp.float32),
+        ],
+        cost_estimate=cost(2 * total * near_rows * width, 20 << 20),
+        compiler_params=params(26, "arbitrary"),
+    )(scalars, *grads, hbm(own), *map(hbm, flat), *map(hbm, theirs), hbm(slope), hbm(obs_t))
+
+
+def settings(numbers, log_rate, copy_from, perturb, devices):
+    members = log_rate.shape[0]
+
+    def kernel(numbers_ref, log_rate_ref, copy_ref, perturb_ref, order_ref, scalars_ref, rate_ref, flag_ref, next_ref):
+        for k in range(devices):
+            order_ref[k] = numbers_ref[k]
+        for k in range(2):
+            scalars_ref[k] = numbers_ref[devices + k]
+        member = numbers_ref[devices + 2]
+        rate_ref[...] = jnp.exp(jnp.full(rate_ref.shape, log_rate_ref[member], jnp.float32))
+        taken = copy_ref[member] == 1
+        flag_ref[0] = taken.astype(jnp.int32)
+        source = jnp.where(taken, lax.rem(member + members - 1, members), member)
+        pick = perturb_ref[member]
+        offset = jnp.where(pick == 0, -0.2, jnp.where(pick == 1, 0.0, 0.2)).astype(jnp.float32)
+        next_ref[...] = jnp.full(next_ref.shape, log_rate_ref[source] + offset, jnp.float32)
+
+    smem = pl.BlockSpec(memory_space=pltpu.SMEM)
+    vmem = pl.BlockSpec(memory_space=pltpu.VMEM)
+    ints = lambda n: jax.ShapeDtypeStruct((n,), jnp.int32)
+    return pl.pallas_call(
+        kernel,
+        name="settings",
+        in_specs=[smem] * 4,
+        out_specs=[smem, smem, vmem, smem, vmem],
+        out_shape=[
+            ints(devices),
+            ints(2),
+            jax.ShapeDtypeStruct((8, 128), jnp.float32),
+            ints(1),
+            jax.ShapeDtypeStruct((1, 1), jnp.float32),
+        ],
+        cost_estimate=cost(1 << 10, 1 << 10),
+        compiler_params=params(4),
+    )(numbers, log_rate, copy_from, perturb)
+
+
+def hub_body(observations, returns, actions, w_input, w_middle, w_head, log_rate, copy_from, perturb):
+    obs, gains, chosen = observations[0], returns[0], actions[0]
+    own_first, own_middle, own_head = w_input[0], w_middle[0], w_head[0]
+    devices = lax.axis_size("dp")
+    half = devices // 4
+    count = 2 * half
+    rows, _ = obs.shape
+    first_rows, width = own_first.shape
+    slab = own_middle.shape[0]
+    acts = own_head.shape[1]
+    pad_acts = -(-(acts + 3) // 32) * 32
+    batch = rows * devices
+    mids = devices * first_rows
+    cut = width // CHUNKS
+    place = lax.axis_index("dp")
+    core = place % 2
+    chip = place // 2
+    high = (chip >= half).astype(jnp.int32)
+    member = lax.axis_index("pop")
+    members = lax.axis_size("pop")
+    ring = [(i, (i + 1) % members) for i in range(members)]
+
+    def side(step, upper):
+        return half + step if upper else half - 1 - step
+
+    def route(step, crossing, back=False):
+        pairs = []
+        for upper in (False, True):
+            hub = side(0, upper != crossing)
+            end = side(step, upper)
+            pairs += [(2 * end + c, 2 * hub + c) for c in range(2)]
+        return [(b, a) for a, b in pairs] if back else pairs
+
+    def near(value, step):
+        return lax.ppermute(value, "dp", route(step, False))
+
+    def far(value, step):
+        return lax.ppermute(value, "dp", route(step, True))
+
+    def outward(value, step):
+        return lax.ppermute(value, "dp", route(step, False, True))
+
+    def partner(value):
+        return lax.ppermute(value, "dp", [(i, i ^ 1) for i in range(devices)])
+
+    def shifted(value):
+        return lax.ppermute(value, "pop", ring)
+
+    slots = jnp.arange(devices, dtype=jnp.int32)
+    upper = high ^ ((slots // half) % 2)
+    order = 2 * jnp.where(upper == 1, half + slots % half, half - 1 - slots % half) + (core ^ (slots // count))
+
+    numbers = jnp.concatenate([order, jnp.stack([core, high, member])]).astype(jnp.int32)
+    order, scalars, rate, flag, next_rate = settings(numbers, log_rate, copy_from, perturb, devices)
+
+    def column(value):
+        out = []
+        for s in range(1, half):
+            out.append(near(value, s))
+        for s in range(half):
+            out.append(far(value, s))
+        return out
+
+    packed = jnp.concatenate(
+        [
+            obs,
+            own_first.reshape(first_rows, devices, slab).swapaxes(0, 1).reshape(-1, slab),
+            jnp.pad(own_head.T, ((0, pad_acts - acts), (0, 0))),
+        ],
+        axis=0,
+    )
+    pieces = [packed] + column(packed)
+    middle_pieces = [column(own_middle[:, q * cut : (q + 1) * cut]) for q in range(CHUNKS)]
+    labels = jnp.stack([gains, chosen.astype(jnp.float32)])
+    labels = jnp.concatenate([labels] + column(labels), axis=1)
+    theirs_small = partner(jnp.stack([p[rows:] for p in pieces]))
+    hidden1, near_t, slope1, obs_t, head = first_layer(order, pieces, theirs_small, rows, slab, half)
+
+    logits = None
+    hidden2, slope2, theirs = None, [], []
+    for q in range(CHUNKS):
+        mine = jnp.concatenate([own_middle[:, q * cut : (q + 1) * cut]] + middle_pieces[q], axis=0)
+        theirs.append(partner(mine))
+        hidden2, slope, logits = second_layer(
+            hidden1, own_middle, middle_pieces[q], theirs[q], head, logits, hidden2, q, cut
+        )
+        slope2.append(slope)
+
+    grad_raw, grad_raw_t, score = policy(logits, labels, acts, batch)
+
+    distance = jnp.where(high == 1, chip - half, half - 1 - chip)
+
+    def home(blocks):
+        out = blocks[0]
+        for s in range(1, half):
+            moved = outward(blocks[s], s)
+            out = jnp.where(distance == s, moved, out)
+        return out
+
+    flag = flag[0] == 1
+
+    near_w = [m[: half - 1] for m in middle_pieces]
+    per = CHUNKS // GROUPS
+    span = per * cut
+    out_middle, grads = [], []
+    for g in range(GROUPS):
+        part = slice(g * per, (g + 1) * per)
+        g2, keep, give = middle_grad(grad_raw, head, slope2[part], near_t, g * per, cut)
+        got = partner(give)
+        new = middle_update(rate, keep, got, own_middle, near_w[part], g, span, cut)
+        new = home(new)
+        moved = shifted(new)
+        out_middle.append(jnp.where(flag, moved, new))
+        grads.append(g2)
+    out_middle = jnp.concatenate(out_middle, axis=1)
+
+    keep, give = input_grad(scalars, grads, own_middle, near_w, theirs, slope1, obs_t, cut)
+    got = far(give, 0)
+    head_term = head_grad(scalars, grad_raw_t, hidden2)
+    mine, sent = gather_small(scalars, order, keep, got, head_term, score, first_rows, slab, half)
+    got = partner(sent)
+    fitness, *new_small = small_update(scalars, rate, mine, got, pieces[:half], score)
+    new_small = home(new_small)
+    fitness = jnp.where(
+        distance == 0, fitness, jnp.sum(new_small[-3:, :1].astype(jnp.float32), axis=0, keepdims=True)
+    )
+    moved = shifted(new_small)
+    out_small = jnp.where(flag, moved, new_small)
+    out_first = out_small[:mids].reshape(devices, first_rows, slab).swapaxes(0, 1).reshape(first_rows, width)
+    out_head = out_small[mids : mids + acts].T
+
+    return (
+        out_first[None],
+        out_middle[None],
+        out_head[None],
+        next_rate.reshape(1),
+        fitness.reshape(1),
+    )
+
+
+def hub_step(*arrays):
+    return hub_body(*arrays)
 
 
 def shifted(block, axis, distance):
     devices = range(lax.axis_size(axis))
     route = [((i - distance) % len(devices), i) for i in devices]
     return lax.ppermute(block, axis, route)
-
-
-def silu_slope(pre):
-    sig = jax.nn.sigmoid(pre)
-    return sig * (1.0 + pre * (1.0 - sig))
-
-
-def contract_rows(left, right):
-    return lax.dot_general(
-        left, right, (((0,), (0,)), ((), ())), preferred_element_type=jnp.float32
-    )
-
-
-def contract_cols(left, right):
-    return lax.dot_general(
-        left, right, (((1,), (1,)), ((), ())), preferred_element_type=jnp.float32
-    )
 
 
 def local(observations, returns, actions, w_input, w_middle, w_head, log_rate, copy_from, perturb):
@@ -125,4 +753,12 @@
         P("pop"),
         P("pop"),
     )
-    return jax.shard_map(local, mesh=mesh, in_specs=in_specs, out_specs=out_specs, check_vma=False)
+
+    def step(*arrays):
+        observations, w_middle = arrays[0], arrays[4]
+        small = observations.shape[1] // 2 <= w_middle.shape[2] and mesh.shape["dp"] % 4 == 0
+        body = hub_step if small else local
+        step = jax.shard_map(body, mesh=mesh, in_specs=in_specs, out_specs=out_specs, check_vma=False)
+        return step(*arrays)
+
+    return step

time: 337 us -> 253 us (0.75)
  waiting for transfers between devices: 229 us -> 59.6 us
  Pallas kernels: 0 us -> 101 us
  starting transfers between devices: 5.14 us -> 71.5 us
  matrix products: 39.2 us -> 0 us
  blocking collectives: 31.2 us -> 0 us
  between operations: 19.1 us -> 4.57 us
  local copies, waits for them, and re-layouts: 6.44 us -> 11.5 us
    pallas_call x0 -> x15, Pallas kernels: none -> 101 us  [the longest x4 38.3 us: second_layer(): pl.pallas_call(kernel, name='second_layer', grid=(total // tile,), in_spe...]
    all_gather x2 -> x0, waiting for transfers between devices: 89.5 us -> none  [the longest x1 79.6 us: local(): lax.all_gather(own_middle, 'dp', axis=0, tiled=True)]
    reduce_scatter x2 -> x0, waiting for transfers between devices: 88.7 us -> none  [the longest x1 88.7 us: local(): lax.psum_scatter(contract_rows(columns, grad_pre2).astype(jnp.bfloat16),...]
    ppermute x3 -> x33, starting transfers between devices: 4.76 us -> 71.5 us  [the longest x13 39.2 us: far(): return lax.ppermute(value, 'dp', route(step, True))]
    dot_general x7 -> x0, matrix products: 39.2 us -> none  [the longest x3 19.2 us: contract_rows(): lax.dot_general(left, right, (((0,), (0,)), ((), ())), preferred_element_...]
    ppermute x3 -> x33, waiting for transfers between devices: 31.4 us -> 59.6 us  [the longest x3 21.7 us: outward(): return lax.ppermute(value, 'dp', route(step, False, True))]
    unnamed x6 -> x0, waiting for transfers between devices: 19.4 us -> none
    all_gather x1 -> x0, blocking collectives: 16 us -> none  [local(): lax.all_gather(own_head, 'dp', axis=0, tiled=True)]
  transfers between devices with their start and end apart: 8 -> 33, of which waited for: 5 -> 8; matrix products, arithmetic and copies ran while one was open for 9% -> 2% of each run, Pallas kernels for 0% -> 33%
where the time goes in v1:
time: 253 us; the launch traced here: 252 us
  Pallas kernels  101 us (40%)
  starting transfers between devices  71.5 us (28%)
  waiting for transfers between devices  59.6 us (24%)
  local copies, waits for them, and re-layouts  11.5 us (5%)
  between operations  4.57 us (2%)
  other arithmetic  4.46 us (2%)
    ppermute x13, starting transfers between devices, far(): return lax.ppermute(value, 'dp', route(step, True))  39.2 us
    pallas_call x4, Pallas kernels, second_layer(): pl.pallas_call(kernel, name='second_layer', grid=(total // tile,), in_spe...  38.3 us
    ppermute x3, waiting for transfers between devices, outward(): return lax.ppermute(value, 'dp', route(step, False, True))  21.7 us
    ppermute x6, starting transfers between devices, near(): return lax.ppermute(value, 'dp', route(step, False))  21.7 us
    ppermute x6, waiting for transfers between devices, near(): return lax.ppermute(value, 'dp', route(step, False))  16.1 us
    ppermute x3, waiting for transfers between devices, shifted(): return lax.ppermute(value, 'pop', ring)  15.9 us
    pallas_call x1, Pallas kernels, input_grad(): pl.pallas_call(kernel, name='input_grad', grid=(total // tile,), in_specs...  15.8 us
    pallas_call x1, Pallas kernels, first_layer(): pl.pallas_call(kernel, name='first_layer', grid_spec=pltpu.PrefetchScalar...  15 us
  transfers between devices with their start and end apart: 33, of which 8 were waited for; matrix products, arithmetic and copies ran while one was open for 2% of the time, Pallas kernels for 33%

profile of v1, /device:TPU:0, one launch (start us, length us, event | category | flops | bytes accessed | tf_op | source)
XLA Modules:
  0.0 252.3 jit_solution(1802023162505983785)
XLA Ops:
  3.4 5.0 %collective-permute-start = (bf16[800,256]{1,0:T(8,128)(2,1)S(1)}, bf16[800,256]{1,0:T(8,128)(2,1)S(1)}, u32[]{:S(2)}, u32[]{:S(2)}) collective-permute-start(bf16[800,256]{1,0:T(8,128)(2,1)S(1)} %pad_maximum_fusion.5.refs_0_), channel_id=1, source_target_pairs={{0,2},{1,3},{6,4},{7,5},{8,10},{9,11},{14,12},{15,13},{16,18},{17,... | collective-permute-start | bytes 1228808 | tf_op jit(solution)/shard_map/ppermute | solution.py:544
  17.2 15.5 %collective-permute-done.16.refs_0_.refs_3_ = bf16[256,512]{1,0:T(8,128)(2,1)S(1)} collective-permute-done((bf16[256,512]{1,0:T(8,128)(2,1)S(1)}, bf16[256,512]{1,0:T(8,128)(2,1)S(1)}, u32[]{:S(2)}, u32[]{:S(2)}) %collective-permute-start.16) | collective-permute-done | bytes 262176 | tf_op jit(solution)/shard_map/ppermute | solution.py:544
  33.4 7.2 %collective-permute-start.12 = (bf16[256,512]{1,0:T(8,128)(2,1)S(1)}, bf16[256,512]{1,0:T(8,128)(2,1)S(1)}, u32[]{:S(2)}, u32[]{:S(2)}) collective-permute-start(bf16[256,512]{1,0:T(8,128)(2,1)S(1)} %get-tuple-element.90), channel_id=1, source_target_pairs={{0,2},{1,3},{6,4},{7,5},{8,10},{9,11},{14,12},{15,13},{16,18},{17,... | collective-permute-start | bytes 786440 | tf_op jit(solution)/shard_map/ppermute | solution.py:544
  41.4 3.8 %collective-permute-start.20 = (f32[2,512]{1,0:T(2,128)S(1)}, f32[2,512]{1,0:T(2,128)S(1)}, u32[]{:S(2)}, u32[]{:S(2)}) collective-permute-start(f32[2,512]{1,0:T(2,128)S(1)} %pad_maximum_fusion.7), channel_id=1, source_target_pairs={{0,2},{1,3},{6,4},{7,5},{8,10},{9,11},{14,12},{15,13},{16,18},{17,... | collective-permute-start | bytes 12296 | tf_op jit(solution)/shard_map/ppermute | solution.py:544
  46.5 5.2 %collective-permute-start.14 = (bf16[256,512]{1,0:T(8,128)(2,1)S(1)}, bf16[256,512]{1,0:T(8,128)(2,1)S(1)}, u32[]{:S(2)}, u32[]{:S(2)}) collective-permute-start(bf16[256,512]{1,0:T(8,128)(2,1)S(1)} %get-tuple-element.90), channel_id=1, source_target_pairs={{0,4},{1,5},{6,2},{7,3},{8,12},{9,13},{14,10},{15,11},{16,20},{17,... | collective-permute-start | bytes 786440 | tf_op jit(solution)/shard_map/ppermute | solution.py:547
  51.6 10.9 %collective-permute-start.22 = (f32[2,512]{1,0:T(2,128)S(1)}, f32[2,512]{1,0:T(2,128)S(1)}, u32[]{:S(2)}, u32[]{:S(2)}) collective-permute-start(f32[2,512]{1,0:T(2,128)S(1)} %pad_maximum_fusion.7), channel_id=1, source_target_pairs={{0,4},{1,5},{6,2},{7,3},{8,12},{9,13},{14,10},{15,11},{16,20},{17,... | collective-permute-start | bytes 12296 | tf_op jit(solution)/shard_map/ppermute | solution.py:547
  64.0 5.0 %collective-permute-start.10 = (bf16[256,512]{1,0:T(8,128)(2,1)S(1)}, bf16[256,512]{1,0:T(8,128)(2,1)S(1)}, u32[]{:S(2)}, u32[]{:S(2)}) collective-permute-start(bf16[256,512]{1,0:T(8,128)(2,1)S(1)} %get-tuple-element.91), channel_id=1, source_target_pairs={{0,4},{1,5},{6,2},{7,3},{8,12},{9,13},{14,10},{15,11},{16,20},{17,... | collective-permute-start | bytes 786440 | tf_op jit(solution)/shard_map/ppermute | solution.py:547
  69.9 3.1 %collective-permute-start.4 = (bf16[256,512]{1,0:T(8,128)(2,1)S(1)}, bf16[256,512]{1,0:T(8,128)(2,1)S(1)}, u32[]{:S(2)}, u32[]{:S(2)}) collective-permute-start(bf16[256,512]{1,0:T(8,128)(2,1)S(1)} %get-tuple-element.92), channel_id=1, source_target_pairs={{0,2},{1,3},{6,4},{7,5},{8,10},{9,11},{14,12},{15,13},{16,18},{17,... | collective-permute-start | bytes 786440 | tf_op jit(solution)/shard_map/ppermute | solution.py:544
  77.0 8.2 %collective-permute-start.6 = (bf16[256,512]{1,0:T(8,128)(2,1)S(1)}, bf16[256,512]{1,0:T(8,128)(2,1)S(1)}, u32[]{:S(2)}, u32[]{:S(2)}) collective-permute-start(bf16[256,512]{1,0:T(8,128)(2,1)S(1)} %get-tuple-element.92), channel_id=1, source_target_pairs={{0,4},{1,5},{6,2},{7,3},{8,12},{9,13},{14,10},{15,11},{16,20},{17,... | collective-permute-start | bytes 786440 | tf_op jit(solution)/shard_map/ppermute | solution.py:547
  90.1 15.0 %first_layer.1 = (bf16[2048,2048]{1,0:T(8,128)(2,1)S(1)}, bf16[1024,2048]{1,0:T(8,128)(2,1)S(1)}, bf16[2048,1024]{1,0:T(8,128)(2,1)}, bf16[256,2048]{1,0:T(8,128)(2,1)}, bf16[32,2048]{1,0:T(8,128)(2,1)S(1)}) custom-call(s32[8]{0:T(128)S(1)} %get-tuple-element.50.order_ref, bf16[800,256]{1,0:T(8,128)(2,1)} %copy-done.7, bf16[800,256]{1,0:T(8,128)(2,1)} %copy-done.20, ...), custom_call_target="tpu_custom_call" | custom-call | flops 4294967296 | bytes 31457280 | tf_op jit(solution)/shard_map/first_layer/pallas_call | solution.py:107
  106.1 9.5 %second_layer.4 = (bf16[2048,2048]{1,0:T(8,128)(2,1)}, bf16[2048,512]{1,0:T(8,128)(2,1)S(1)}, f32[2048,32]{1,0:T(8,128)S(1)}) custom-call(bf16[2048,2048]{1,0:T(8,128)(2,1)S(1)} %get-tuple-element.51.h1_ref, bf16[256,2048]{1,0:T(8,128)(2,1)} %bitcast.36, bf16[256,512]{1,0:T(8,128)(2,1)} %copy-done.19, bf16[256,512]{1,0:T(8,128)(2,1)} %copy-done.25, ...), custom_call_target="tpu_custom_call" | custom-call | flops 4294967296 | bytes 16777216 | tf_op jit(solution)/shard_map/second_layer/pallas_call | solution.py:167
  116.6 9.6 %second_layer.5 = (bf16[2048,2048]{1,0:T(8,128)(2,1)}, bf16[2048,512]{1,0:T(8,128)(2,1)S(1)}, f32[2048,32]{1,0:T(8,128)S(1)}) custom-call(bf16[2048,2048]{1,0:T(8,128)(2,1)S(1)} %get-tuple-element.51.h1_ref, bf16[256,2048]{1,0:T(8,128)(2,1)} %bitcast.37, bf16[256,512]{1,0:T(8,128)(2,1)} %copy-done.5, ...), custom_call_target="tpu_custom_call", output_to_operand_aliasing={{0}: (8, {})} | custom-call | flops 4294967296 | bytes 16777216 | tf_op jit(solution)/shard_map/second_layer/pallas_call | solution.py:167
  127.2 9.6 %second_layer.6 = (bf16[2048,2048]{1,0:T(8,128)(2,1)}, bf16[2048,512]{1,0:T(8,128)(2,1)S(1)}, f32[2048,32]{1,0:T(8,128)S(1)}) custom-call(bf16[2048,2048]{1,0:T(8,128)(2,1)S(1)} %get-tuple-element.51.h1_ref, bf16[256,2048]{1,0:T(8,128)(2,1)} %bitcast.38, bf16[256,512]{1,0:T(8,128)(2,1)} %copy-done.4, ...), custom_call_target="tpu_custom_call", output_to_operand_aliasing={{0}: (8, {})} | custom-call | flops 4294967296 | bytes 16777216 | tf_op jit(solution)/shard_map/second_layer/pallas_call | solution.py:167
  137.8 9.6 %second_layer.7 = (bf16[2048,2048]{1,0:T(8,128)(2,1)}, bf16[2048,512]{1,0:T(8,128)(2,1)S(1)}, f32[2048,32]{1,0:T(8,128)S(1)}) custom-call(bf16[2048,2048]{1,0:T(8,128)(2,1)S(1)} %get-tuple-element.51.h1_ref, bf16[256,2048]{1,0:T(8,128)(2,1)} %bitcast.39, bf16[256,512]{1,0:T(8,128)(2,1)} %copy-done.6, ...), custom_call_target="tpu_custom_call", output_to_operand_aliasing={{0}: (8, {})} | custom-call | flops 4294967296 | bytes 16777216 | tf_op jit(solution)/shard_map/second_layer/pallas_call | solution.py:167
  148.3 7.4 %middle_grad.2 = (bf16[2048,1024]{1,0:T(8,128)(2,1)S(1)}, f32[512,1024]{1,0:T(8,128)S(1)}, bf16[512,1024]{1,0:T(8,128)(2,1)}) custom-call(bf16[2048,32]{1,0:T(8,128)(2,1)S(1)} %get-tuple-element.60.graw_ref, bf16[32,2048]{1,0:T(8,128)(2,1)S(1)} %get-tuple-element.52.refs_4_.head_ref, bf16[2048,512]{1,0:T(8,128)(2,1)S(1)} %get-tuple-element.61.refs_0_, ...), custom_call_target="tpu_custom_call" | custom-call | flops 4294967296 | bytes 16777216 | tf_op jit(solution)/shard_map/middle_grad/pallas_call | solution.py:254
  156.2 7.4 %middle_grad.3 = (bf16[2048,1024]{1,0:T(8,128)(2,1)S(1)}, f32[512,1024]{1,0:T(8,128)S(1)}, bf16[512,1024]{1,0:T(8,128)(2,1)}) custom-call(bf16[2048,32]{1,0:T(8,128)(2,1)S(1)} %get-tuple-element.60.graw_ref, bf16[32,2048]{1,0:T(8,128)(2,1)S(1)} %get-tuple-element.52.refs_4_.head_ref, bf16[2048,512]{1,0:T(8,128)(2,1)S(1)} %get-tuple-element.65.refs_0_, ...), custom_call_target="tpu_custom_call" | custom-call | flops 4294967296 | bytes 16777216 | tf_op jit(solution)/shard_map/middle_grad/pallas_call | solution.py:254
  163.7 15.8 %input_grad.1 = (bf16[128,1024]{1,0:T(8,128)(2,1)S(1)}, bf16[128,1024]{1,0:T(8,128)(2,1)}) custom-call(s32[2]{0:T(128)S(1)} %get-tuple-element.48.scalar_ref, bf16[2048,1024]{1,0:T(8,128)(2,1)S(1)} %get-tuple-element.64.refs_0_, bf16[2048,1024]{1,0:T(8,128)(2,1)S(1)} %get-tuple-element.67.refs_1_, bf16[256,2048]{1,0:T(8,128)(2,1)} %bitcast.40, ...), custom_call_target="tpu_custom_call" | custom-call | flops 8589934592 | bytes 20971520 | tf_op jit(solution)/shard_map/input_grad/pallas_call | solution.py:449
  180.2 3.3 %head_grad.1.side_ref = f32[32,1024]{1,0:T(8,128)S(1)} custom-call(s32[2]{0:T(128)S(1)} %get-tuple-element.48.scalar_ref, bf16[32,2048]{1,0:T(8,128)(2,1)S(1)} %get-tuple-element.72.graw_t_ref, bf16[2048,2048]{1,0:T(8,128)(2,1)} %get-tuple-element.73.h2_ref), custom_call_target="tpu_custom_call" | custom-call | flops 1073741824 | bytes 6291456 | tf_op jit(solution)/shard_map/head_grad/pallas_call | solution.py:284
  188.0 3.0 %middle_update.2 = (bf16[256,1024]{1,0:T(8,128)(2,1)}, bf16[256,1024]{1,0:T(8,128)(2,1)}) custom-call(f32[8,128]{1,0:T(8,128)S(1)} %get-tuple-element.49.rate_ref, f32[512,1024]{1,0:T(8,128)S(1)} %get-tuple-element.79.keep_ref, bf16[512,1024]{1,0:T(8,128)(2,1)} %copy-done.18, bf16[256,2048]{1,0:T(8,128)(2,1)} %bitcast.41, bf16[256,512]{1,0:T(8,128)(2,1)} %copy-done.19, ...), custom_call_target="tpu_custom_call" | custom-call | flops 134217728 | bytes 4194304 | tf_op jit(solution)/shard_map/middle_update/pallas_call | solution.py:318
  198.8 3.1 %middle_update.3 = (bf16[256,1024]{1,0:T(8,128)(2,1)}, bf16[256,1024]{1,0:T(8,128)(2,1)}) custom-call(f32[8,128]{1,0:T(8,128)S(1)} %get-tuple-element.49.rate_ref, f32[512,1024]{1,0:T(8,128)S(1)} %get-tuple-element.83.keep_ref, bf16[512,1024]{1,0:T(8,128)(2,1)} %copy-done.17, bf16[256,2048]{1,0:T(8,128)(2,1)} %bitcast.42, bf16[256,512]{1,0:T(8,128)(2,1)} %copy-done.4, ...), custom_call_target="tpu_custom_call" | custom-call | flops 134217728 | bytes 4194304 | tf_op jit(solution)/shard_map/middle_update/pallas_call | solution.py:318
  203.3 16.8 %collective-permute-done.25 = bf16[288,256]{1,0:T(8,128)(2,1)S(1)} collective-permute-done((bf16[288,256]{1,0:T(8,128)(2,1)}, bf16[288,256]{1,0:T(8,128)(2,1)S(1)}, u32[]{:S(2)}, u32[]{:S(2)}) %collective-permute-start.25) | collective-permute-done | bytes 147488 | tf_op jit(solution)/shard_map/ppermute | solution.py:550
  226.1 4.9 %collective-permute-done.31 = bf16[256,1024]{1,0:T(8,128)(2,1)S(1)} collective-permute-done((bf16[256,1024]{1,0:T(8,128)(2,1)}, bf16[256,1024]{1,0:T(8,128)(2,1)S(1)}, u32[]{:S(2)}, u32[]{:S(2)}) %collective-permute-start.31) | collective-permute-done | bytes 524320 | tf_op jit(solution)/shard_map/ppermute | solution.py:550
  234.2 6.2 %collective-permute-done.29 = bf16[256,1024]{1,0:T(8,128)(2,1)S(1)} collective-permute-done((bf16[256,1024]{1,0:T(8,128)(2,1)S(1)}, bf16[256,1024]{1,0:T(8,128)(2,1)S(1)}, u32[]{:S(2)}, u32[]{:S(2)}) %collective-permute-start.29) | collective-permute-done | bytes 524320 | tf_op jit(solution)/shard_map/ppermute | solution.py:556
  240.4 9.7 %collective-permute-done.32 = bf16[256,1024]{1,0:T(8,128)(2,1)S(1)} collective-permute-done((bf16[256,1024]{1,0:T(8,128)(2,1)S(1)}, bf16[256,1024]{1,0:T(8,128)(2,1)S(1)}, u32[]{:S(2)}, u32[]{:S(2)}) %collective-permute-start.32) | collective-permute-done | bytes 524320 | tf_op jit(solution)/shard_map/ppermute | solution.py:556
  (156 shorter events, 53.1 us)
Async XLA Ops:
  3.4 37.9 %collective-permute-start = (bf16[800,256]{1,0:T(8,128)(2,1)S(1)}, bf16[800,256]{1,0:T(8,128)(2,1)S(1)}, u32[]{:S(2)}, u32[]{:S(2)}) collective-permute-start(bf16[800,256]{1,0:T(8,128)(2,1)S(1)} %pad_maximum_fusion.5.refs_0_), channel_id=1, source_target_pairs={{0,2},{1,3},{6,4},{7,5},{8,10},{9,11},{14,12},{15,13},{16,18},{17,... | collective-permute-start | bytes 1228808 | tf_op jit(solution)/shard_map/ppermute | solution.py:544
  8.4 36.7 %collective-permute-start.2 = (bf16[800,256]{1,0:T(8,128)(2,1)S(1)}, bf16[800,256]{1,0:T(8,128)(2,1)S(1)}, u32[]{:S(2)}, u32[]{:S(2)}) collective-permute-start(bf16[800,256]{1,0:T(8,128)(2,1)S(1)} %pad_maximum_fusion.5.refs_0_), channel_id=1, source_target_pairs={{0,4},{1,5},{6,2},{7,3},{8,12},{9,13},{14,10},{15,11},{16,20},{17,... | collective-permute-start | bytes 1228808 | tf_op jit(solution)/shard_map/ppermute | solution.py:547
  10.8 21.9 %collective-permute-start.16 = (bf16[256,512]{1,0:T(8,128)(2,1)S(1)}, bf16[256,512]{1,0:T(8,128)(2,1)S(1)}, u32[]{:S(2)}, u32[]{:S(2)}) collective-permute-start(bf16[256,512]{1,0:T(8,128)(2,1)S(1)} %get-tuple-element.89), channel_id=1, source_target_pairs={{0,2},{1,3},{6,4},{7,5},{8,10},{9,11},{14,12},{15,13},{16,18},{17,... | collective-permute-start | bytes 786440 | tf_op jit(solution)/shard_map/ppermute | solution.py:544
  12.2 21.2 %collective-permute-start.17 = (bf16[256,512]{1,0:T(8,128)(2,1)S(1)}, bf16[256,512]{1,0:T(8,128)(2,1)S(1)}, u32[]{:S(2)}, u32[]{:S(2)}) collective-permute-start(bf16[256,512]{1,0:T(8,128)(2,1)S(1)} %get-tuple-element.89), channel_id=1, source_target_pairs={{2,4},{3,5},{4,2},{5,3},{10,12},{11,13},{12,10},{13,11},{18,20},{1... | collective-permute-start | bytes 786440 | tf_op jit(solution)/shard_map/ppermute | solution.py:547
  12.8 27.7 %collective-permute-start.18 = (bf16[256,512]{1,0:T(8,128)(2,1)S(1)}, bf16[256,512]{1,0:T(8,128)(2,1)S(1)}, u32[]{:S(2)}, u32[]{:S(2)}) collective-permute-start(bf16[256,512]{1,0:T(8,128)(2,1)S(1)} %get-tuple-element.89), channel_id=1, source_target_pairs={{0,4},{1,5},{6,2},{7,3},{8,12},{9,13},{14,10},{15,11},{16,20},{17,... | collective-permute-start | bytes 786440 | tf_op jit(solution)/shard_map/ppermute | solution.py:547
  32.7 29.9 %collective-permute-start.1 = (bf16[800,256]{1,0:T(8,128)(2,1)S(1)}, bf16[800,256]{1,0:T(8,128)(2,1)S(1)}, u32[]{:S(2)}, u32[]{:S(2)}) collective-permute-start(bf16[800,256]{1,0:T(8,128)(2,1)S(1)} %pad_maximum_fusion.5.refs_0_), channel_id=1, source_target_pairs={{2,4},{3,5},{4,2},{5,3},{10,12},{11,13},{12,10},{13,11},{18,20},{1... | collective-permute-start | bytes 1228808 | tf_op jit(solution)/shard_map/ppermute | solution.py:547
  33.4 35.6 %collective-permute-start.12 = (bf16[256,512]{1,0:T(8,128)(2,1)S(1)}, bf16[256,512]{1,0:T(8,128)(2,1)S(1)}, u32[]{:S(2)}, u32[]{:S(2)}) collective-permute-start(bf16[256,512]{1,0:T(8,128)(2,1)S(1)} %get-tuple-element.90), channel_id=1, source_target_pairs={{0,2},{1,3},{6,4},{7,5},{8,10},{9,11},{14,12},{15,13},{16,18},{17,... | collective-permute-start | bytes 786440 | tf_op jit(solution)/shard_map/ppermute | solution.py:544
  40.6 29.1 %collective-permute-start.13 = (bf16[256,512]{1,0:T(8,128)(2,1)S(1)}, bf16[256,512]{1,0:T(8,128)(2,1)S(1)}, u32[]{:S(2)}, u32[]{:S(2)}) collective-permute-start(bf16[256,512]{1,0:T(8,128)(2,1)S(1)} %get-tuple-element.90), channel_id=1, source_target_pairs={{2,4},{3,5},{4,2},{5,3},{10,12},{11,13},{12,10},{13,11},{18,20},{1... | collective-permute-start | bytes 786440 | tf_op jit(solution)/shard_map/ppermute | solution.py:547
  46.5 23.4 %collective-permute-start.14 = (bf16[256,512]{1,0:T(8,128)(2,1)S(1)}, bf16[256,512]{1,0:T(8,128)(2,1)S(1)}, u32[]{:S(2)}, u32[]{:S(2)}) collective-permute-start(bf16[256,512]{1,0:T(8,128)(2,1)S(1)} %get-tuple-element.90), channel_id=1, source_target_pairs={{0,4},{1,5},{6,2},{7,3},{8,12},{9,13},{14,10},{15,11},{16,20},{17,... | collective-permute-start | bytes 786440 | tf_op jit(solution)/shard_map/ppermute | solution.py:547
  51.6 12.4 %collective-permute-start.22 = (f32[2,512]{1,0:T(2,128)S(1)}, f32[2,512]{1,0:T(2,128)S(1)}, u32[]{:S(2)}, u32[]{:S(2)}) collective-permute-start(f32[2,512]{1,0:T(2,128)S(1)} %pad_maximum_fusion.7), channel_id=1, source_target_pairs={{0,4},{1,5},{6,2},{7,3},{8,12},{9,13},{14,10},{15,11},{16,20},{17,... | collective-permute-start | bytes 12296 | tf_op jit(solution)/shard_map/ppermute | solution.py:547
  69.7 35.4 %collective-permute-start.19 = (bf16[1024,512]{1,0:T(8,128)(2,1)S(1)}, bf16[1024,512]{1,0:T(8,128)(2,1)S(1)}, u32[]{:S(2)}, u32[]{:S(2)}) collective-permute-start(bf16[1024,512]{1,0:T(8,128)(2,1)S(1)} %pad_maximum_fusion.3), channel_id=1, source_target_pairs={{0,1},{1,0},{2,3},{3,2},{4,5},{5,4},{6,7},{7,6},{8,9},{9,8},{10,11... | collective-permute-start | bytes 3145736 | tf_op jit(solution)/shard_map/ppermute | solution.py:553
  69.9 15.4 %collective-permute-start.4 = (bf16[256,512]{1,0:T(8,128)(2,1)S(1)}, bf16[256,512]{1,0:T(8,128)(2,1)S(1)}, u32[]{:S(2)}, u32[]{:S(2)}) collective-permute-start(bf16[256,512]{1,0:T(8,128)(2,1)S(1)} %get-tuple-element.92), channel_id=1, source_target_pairs={{0,2},{1,3},{6,4},{7,5},{8,10},{9,11},{14,12},{15,13},{16,18},{17,... | collective-permute-start | bytes 786440 | tf_op jit(solution)/shard_map/ppermute | solution.py:544
  73.0 16.2 %collective-permute-start.3 = (bf16[4,288,256]{2,1,0:T(8,128)(2,1)S(1)}, bf16[4,288,256]{2,1,0:T(8,128)(2,1)S(1)}, u32[]{:S(2)}, u32[]{:S(2)}) collective-permute-start(bf16[4,288,256]{2,1,0:T(8,128)(2,1)S(1)} %pad_maximum_fusion.4), channel_id=1, source_target_pairs={{0,1},{1,0},{2,3},{3,2},{4,5},{5,4},{6,7},{7,6},{8,9},{9,8},{10,11... | collective-permute-start | bytes 1769480 | tf_op jit(solution)/shard_map/ppermute | solution.py:553
  85.3 30.3 %collective-permute-start.15 = (bf16[1024,512]{1,0:T(8,128)(2,1)S(1)}, bf16[1024,512]{1,0:T(8,128)(2,1)S(1)}, u32[]{:S(2)}, u32[]{:S(2)}) collective-permute-start(bf16[1024,512]{1,0:T(8,128)(2,1)S(1)} %pad_maximum_fusion.2), channel_id=1, source_target_pairs={{0,1},{1,0},{2,3},{3,2},{4,5},{5,4},{6,7},{7,6},{8,9},{9,8},{10,11... | collective-permute-start | bytes 3145736 | tf_op jit(solution)/shard_map/ppermute | solution.py:553
  85.6 40.7 %collective-permute-start.11 = (bf16[1024,512]{1,0:T(8,128)(2,1)S(1)}, bf16[1024,512]{1,0:T(8,128)(2,1)S(1)}, u32[]{:S(2)}, u32[]{:S(2)}) collective-permute-start(bf16[1024,512]{1,0:T(8,128)(2,1)S(1)} %pad_maximum_fusion.1), channel_id=1, source_target_pairs={{0,1},{1,0},{2,3},{3,2},{4,5},{5,4},{6,7},{7,6},{8,9},{9,8},{10,11... | collective-permute-start | bytes 3145736 | tf_op jit(solution)/shard_map/ppermute | solution.py:553
  89.2 47.6 %collective-permute-start.7 = (bf16[1024,512]{1,0:T(8,128)(2,1)S(1)}, bf16[1024,512]{1,0:T(8,128)(2,1)S(1)}, u32[]{:S(2)}, u32[]{:S(2)}) collective-permute-start(bf16[1024,512]{1,0:T(8,128)(2,1)S(1)} %pad_maximum_fusion), channel_id=1, source_target_pairs={{0,1},{1,0},{2,3},{3,2},{4,5},{5,4},{6,7},{7,6},{8,9},{9,8},{10,11... | collective-permute-start | bytes 3145736 | tf_op jit(solution)/shard_map/ppermute | solution.py:553
  155.7 31.3 %collective-permute-start.27 = (bf16[512,1024]{1,0:T(8,128)(2,1)}, bf16[512,1024]{1,0:T(8,128)(2,1)S(1)}, u32[]{:S(2)}, u32[]{:S(2)}) collective-permute-start(bf16[512,1024]{1,0:T(8,128)(2,1)} %get-tuple-element.80), channel_id=1, source_target_pairs={{0,1},{1,0},{2,3},{3,2},{4,5},{5,4},{6,7},{7,6},{8,9},{9,8},{10,11... | collective-permute-start | bytes 3145736 | tf_op jit(solution)/shard_map/ppermute | solution.py:553
  163.7 34.1 %collective-permute-start.30 = (bf16[512,1024]{1,0:T(8,128)(2,1)}, bf16[512,1024]{1,0:T(8,128)(2,1)S(1)}, u32[]{:S(2)}, u32[]{:S(2)}) collective-permute-start(bf16[512,1024]{1,0:T(8,128)(2,1)} %get-tuple-element.84), channel_id=1, source_target_pairs={{0,1},{1,0},{2,3},{3,2},{4,5},{5,4},{6,7},{7,6},{8,9},{9,8},{10,11... | collective-permute-start | bytes 3145736 | tf_op jit(solution)/shard_map/ppermute | solution.py:553
  191.1 32.4 %collective-permute-start.28 = (bf16[256,1024]{1,0:T(8,128)(2,1)}, bf16[256,1024]{1,0:T(8,128)(2,1)}, u32[]{:S(2)}, u32[]{:S(2)}) collective-permute-start(bf16[256,1024]{1,0:T(8,128)(2,1)} %get-tuple-element.81), channel_id=1, source_target_pairs={{2,0},{3,1},{4,6},{5,7},{10,8},{11,9},{12,14},{13,15},{18,16},{19,... | collective-permute-start | bytes 1572872 | tf_op jit(solution)/shard_map/ppermute | solution.py:550
  195.8 24.2 %collective-permute-start.25 = (bf16[288,256]{1,0:T(8,128)(2,1)}, bf16[288,256]{1,0:T(8,128)(2,1)S(1)}, u32[]{:S(2)}, u32[]{:S(2)}) collective-permute-start(bf16[288,256]{1,0:T(8,128)(2,1)} %get-tuple-element.77), channel_id=1, source_target_pairs={{2,0},{3,1},{4,6},{5,7},{10,8},{11,9},{12,14},{13,15},{18,16},{19,... | collective-permute-start | bytes 442376 | tf_op jit(solution)/shard_map/ppermute | solution.py:550
  201.8 29.2 %collective-permute-start.31 = (bf16[256,1024]{1,0:T(8,128)(2,1)}, bf16[256,1024]{1,0:T(8,128)(2,1)S(1)}, u32[]{:S(2)}, u32[]{:S(2)}) collective-permute-start(bf16[256,1024]{1,0:T(8,128)(2,1)} %get-tuple-element.85), channel_id=1, source_target_pairs={{2,0},{3,1},{4,6},{5,7},{10,8},{11,9},{12,14},{13,15},{18,16},{19,... | collective-permute-start | bytes 1572872 | tf_op jit(solution)/shard_map/ppermute | solution.py:550
  220.1 12.6 %collective-permute-start.26 = (bf16[288,256]{1,0:T(8,128)(2,1)S(1)}, bf16[288,256]{1,0:T(8,128)(2,1)S(1)}, u32[]{:S(2)}, u32[]{:S(2)}) collective-permute-start(bf16[288,256]{1,0:T(8,128)(2,1)S(1)} %broadcast_select_fusion.4), channel_id=1, source_target_pairs={{0,8},{8,16},{16,24},{24,0},{1,9},{9,17},{17,25},{25,1},{2,10},{10... | collective-permute-start | bytes 442376 | tf_op jit(solution)/shard_map/ppermute | solution.py:556
  224.6 15.7 %collective-permute-start.29 = (bf16[256,1024]{1,0:T(8,128)(2,1)S(1)}, bf16[256,1024]{1,0:T(8,128)(2,1)S(1)}, u32[]{:S(2)}, u32[]{:S(2)}) collective-permute-start(bf16[256,1024]{1,0:T(8,128)(2,1)S(1)} %broadcast_select_fusion.1), channel_id=1, source_target_pairs={{0,8},{8,16},{16,24},{24,0},{1,9},{9,17},{17,25},{25,1},{2,10},{10... | collective-permute-start | bytes 1572872 | tf_op jit(solution)/shard_map/ppermute | solution.py:556
  231.2 18.9 %collective-permute-start.32 = (bf16[256,1024]{1,0:T(8,128)(2,1)S(1)}, bf16[256,1024]{1,0:T(8,128)(2,1)S(1)}, u32[]{:S(2)}, u32[]{:S(2)}) collective-permute-start(bf16[256,1024]{1,0:T(8,128)(2,1)S(1)} %broadcast_select_fusion), channel_id=1, source_target_pairs={{0,8},{8,16},{16,24},{24,0},{1,9},{9,17},{17,25},{25,1},{2,10},{10... | collective-permute-start | bytes 1572872 | tf_op jit(solution)/shard_map/ppermute | solution.py:556
  (43 other events, 610.6 us)

commit v2 on v1

--- a/solution.py
+++ b/solution.py
@@ -6,7 +6,7 @@
 from jax.sharding import PartitionSpec as P
 
 CAP = 2.0
-CHUNKS = 4
+PARTS = (2, 2)
 GROUPS = 2
 
 
@@ -51,13 +51,54 @@
     return pl.CostEstimate(flops=int(flops), bytes_accessed=int(moved), transcendentals=0)
 
 
-def first_layer(order, pieces, theirs, rows, slab, near_blocks):
+def pack(obs, first, head, gains, chosen, slab, pad_acts):
+    rows, features = obs.shape
+    each, width = first.shape
+    devices = width // slab
+    acts = head.shape[1]
+    mids = devices * each
+    per = rows // features
+    at = rows + mids + pad_acts
+    total = at + -(-4 * per // 16) * 16
+
+    def kernel(obs_ref, first_ref, head_ref, gains_ref, chosen_ref, out_ref):
+        out_ref[:rows, :] = obs_ref[...]
+        for b in range(devices):
+            out_ref[rows + b * each : rows + (b + 1) * each, :] = first_ref[:, b * slab : (b + 1) * slab]
+        block = head_ref[...].astype(jnp.float32)
+        block = jnp.concatenate([block, jnp.zeros((slab, 128 - acts), jnp.float32)], axis=1)
+        out_ref[rows + mids : at, :] = block.T[:pad_acts].astype(jnp.bfloat16)
+        out_ref[at:, :] = jnp.zeros((total - at, features), jnp.bfloat16)
+        value = gains_ref[...]
+        parts = []
+        for _ in range(3):
+            parts.append(value.astype(jnp.bfloat16))
+            value = value - parts[-1].astype(jnp.float32)
+        parts.append(chosen_ref[...].astype(jnp.float32).astype(jnp.bfloat16))
+        for t, part in enumerate(parts):
+            for r in range(per):
+                row = at + t * per + r
+                out_ref[row : row + 1, :] = part[:, r * features : (r + 1) * features]
+
+    arrays = (obs, first, head, gains, chosen)
+    return pl.pallas_call(
+        kernel,
+        name="pack",
+        grid=(1,),
+        in_specs=[whole(v) for v in arrays],
+        out_specs=pl.BlockSpec((total, features), lambda i: (0, 0)),
+        out_shape=pltpu.HBM((total, features), jnp.bfloat16),
+        cost_estimate=cost(1 << 24, 1 << 20),
+        compiler_params=params(6, "arbitrary"),
+    )(*map(hbm, arrays))
+
+
+def first_layer(order, scalars, pieces, theirs, rows, slab, near_blocks, pad_acts):
     count = len(pieces)
     devices = 2 * count
     features = pieces[0].shape[1]
     each = features // devices
     mids = devices * each
-    pad_acts = pieces[0].shape[0] - rows - mids
     width = devices * slab
     total = count * rows
     near_all = 2 * near_blocks
@@ -65,7 +106,8 @@
     def near_at(i):
         return (i // count) * near_blocks + jnp.minimum(i % count, near_blocks - 1)
 
-    def kernel(order_ref, *refs):
+    def kernel(order_ref, scalar_ref, *refs):
+        live = scalar_ref[2] == 1
         piece_refs, theirs_ref = refs[:count], refs[count]
         h1_ref, h1t_ref, slope_ref, obst_ref, head_ref, cols = refs[count + 1 :]
         i = pl.program_id(0)
@@ -75,7 +117,7 @@
                 return piece_refs[k][pl.ds(rows + start, size), :]
             return theirs_ref[k - count, pl.ds(start, size), :]
 
-        @pl.when(i == 0)
+        @pl.when(live & (i == 0))
         def _():
             for k in range(devices):
                 at = pl.multiple_of(order_ref[k] * each, each)
@@ -88,35 +130,42 @@
                 block = piece_refs[p][:rows, :].astype(jnp.float32)
                 obst_ref[:, p * rows : (p + 1) * rows] = block.T.astype(jnp.bfloat16)
 
-        weights = cols[i]
-        for p in range(count):
-            pre = dot(piece_refs[p][:rows, :], weights)
-            h1_ref[p * rows : (p + 1) * rows, :] = (pre * sigmoid(pre)).astype(jnp.bfloat16)
-
-        @pl.when(i % count < near_blocks)
-        def _():
+        close = i % count < near_blocks
+
+        @pl.when(live & close)
+        def _():
+            weights = cols[i]
             for p in range(count):
+                at = slice(p * rows, (p + 1) * rows)
                 obs = piece_refs[p][:rows, :]
                 pre = dot(obs, weights)
                 sig = sigmoid(pre)
-                slope_ref[p * rows : (p + 1) * rows, :] = (sig * (1.0 + pre * (1.0 - sig))).astype(jnp.bfloat16)
+                h1_ref[at, :] = (pre * sig).astype(jnp.bfloat16)
+                slope_ref[at, :] = (sig * (1.0 + pre * (1.0 - sig))).astype(jnp.bfloat16)
                 pre_t = dot(weights, obs, ((0,), (1,)))
-                h1t_ref[:, p * rows : (p + 1) * rows] = (pre_t * sigmoid(pre_t)).astype(jnp.bfloat16)
+                h1t_ref[:, at] = (pre_t * sigmoid(pre_t)).astype(jnp.bfloat16)
+
+        @pl.when(live & jnp.logical_not(close))
+        def _():
+            weights = cols[i]
+            for p in range(count):
+                pre = dot(piece_refs[p][:rows, :], weights)
+                h1_ref[p * rows : (p + 1) * rows, :] = (pre * sigmoid(pre)).astype(jnp.bfloat16)
 
     shape = lambda *s: jax.ShapeDtypeStruct(s, jnp.bfloat16)
     return pl.pallas_call(
         kernel,
         name="first_layer",
         grid_spec=pltpu.PrefetchScalarGridSpec(
-            num_scalar_prefetch=1,
+            num_scalar_prefetch=2,
             grid=(devices,),
             in_specs=[whole(p) for p in pieces] + [whole(theirs)],
             out_specs=[
-                pl.BlockSpec((total, slab), lambda i, _: (0, i)),
-                pl.BlockSpec((slab, total), lambda i, _: (near_at(i), 0)),
-                pl.BlockSpec((total, slab), lambda i, _: (0, near_at(i))),
-                pl.BlockSpec((features, total), lambda i, _: (0, 0)),
-                pl.BlockSpec((pad_acts, width), lambda i, _: (0, 0)),
+                pl.BlockSpec((total, slab), lambda i, *_: (0, i)),
+                pl.BlockSpec((slab, total), lambda i, *_: (near_at(i), 0)),
+                pl.BlockSpec((total, slab), lambda i, *_: (0, near_at(i))),
+                pl.BlockSpec((features, total), lambda i, *_: (0, 0)),
+                pl.BlockSpec((pad_acts, width), lambda i, *_: (0, 0)),
             ],
             scratch_shapes=[pltpu.VMEM((devices, features, slab), jnp.bfloat16)],
         ),
@@ -129,48 +178,52 @@
         ],
         cost_estimate=cost(2 * total * features * width * 2, 30 << 20),
         compiler_params=params(20, "arbitrary"),
-    )(order, *map(hbm, pieces), hbm(theirs))
-
-
-def second_layer(hidden1, own, pieces, theirs, head, logits, hidden2, q, cut):
+    )(order, scalars, *map(hbm, pieces), theirs)
+
+
+def second_layer(scalars, hidden1, own, pieces, theirs, head, logits, hidden2, start, inner, cut):
     total, width = hidden1.shape
     slab = own.shape[0]
     pad_acts = head.shape[0]
     tile = min(512, total)
     first = logits is None
     sub = 256
-
-    def kernel(h1_ref, own_ref, *refs):
+    q = start // cut
+
+    def kernel(scalar_ref, h1_ref, own_ref, *refs):
+        live = scalar_ref[2] == 1
         piece_refs = refs[: len(pieces)]
         theirs_ref, head_ref = refs[len(pieces) : len(pieces) + 2]
         rest = refs[len(pieces) + 2 :]
         logits_in = None if first else rest[0]
         h2_ref, slope_ref, logits_ref, weights = rest[0 if first else 2 :]
 
-        @pl.when(pl.program_id(0) == 0)
+        @pl.when(live & (pl.program_id(0) == 0))
         def _():
             weights[:slab] = own_ref[...]
             for k, piece in enumerate(piece_refs):
                 weights[(k + 1) * slab : (k + 2) * slab] = piece[...]
             weights[(len(pieces) + 1) * slab :] = theirs_ref[...]
 
-        for r in range(0, tile, sub):
-            pre = dot(h1_ref[r : r + sub, :], weights[...])
-            sig = sigmoid(pre)
-            hidden = (pre * sig).astype(jnp.bfloat16)
-            h2_ref[r : r + sub, :] = hidden
-            slope_ref[r : r + sub, :] = (sig * (1.0 + pre * (1.0 - sig))).astype(jnp.bfloat16)
-            part = dot(hidden, head_ref[...], ((1,), (1,)))
-            logits_ref[r : r + sub, :] = part if first else part + logits_in[r : r + sub, :]
+        @pl.when(live)
+        def _():
+            for r in range(0, tile, sub):
+                pre = dot(h1_ref[r : r + sub, :], weights[...])
+                sig = sigmoid(pre)
+                hidden = (pre * sig).astype(jnp.bfloat16)
+                h2_ref[r : r + sub, :] = hidden
+                slope_ref[r : r + sub, :] = (sig * (1.0 + pre * (1.0 - sig))).astype(jnp.bfloat16)
+                part = dot(hidden, head_ref[...], ((1,), (1,)))
+                logits_ref[r : r + sub, :] = part if first else part + logits_in[r : r + sub, :]
 
     row = lambda size: pl.BlockSpec((tile, size), lambda i: (i, 0))
     return pl.pallas_call(
         kernel,
         name="second_layer",
         grid=(total // tile,),
-        in_specs=[row(width), pl.BlockSpec((slab, cut), lambda i: (0, q))]
-        + [whole(p) for p in pieces]
-        + [whole(theirs), pl.BlockSpec((pad_acts, cut), lambda i: (0, q))]
+        in_specs=[pl.BlockSpec(memory_space=pltpu.SMEM), row(width), pl.BlockSpec((slab, cut), lambda i: (0, q))]
+        + [pl.BlockSpec((slab, cut), lambda i: (0, inner))] * len(pieces)
+        + [pl.BlockSpec((theirs.shape[0], cut), lambda i: (0, inner)), pl.BlockSpec((pad_acts, cut), lambda i: (0, q))]
         + ([] if first else [row(pad_acts), pl.BlockSpec(memory_space=pltpu.HBM)]),
         out_specs=[pl.BlockSpec((tile, cut), lambda i: (i, q)), row(cut), row(pad_acts)],
         out_shape=[
@@ -179,18 +232,28 @@
             jax.ShapeDtypeStruct((total, pad_acts), jnp.float32),
         ],
         scratch_shapes=[pltpu.VMEM((width, cut), jnp.bfloat16)],
-        input_output_aliases={} if first else {len(pieces) + 5: 0},
+        input_output_aliases={} if first else {len(pieces) + 6: 0},
         cost_estimate=cost(2 * total * width * cut, 16 << 20),
-        compiler_params=params(18, "arbitrary"),
-    )(hidden1, hbm(own), *map(hbm, pieces), hbm(theirs), head, *([] if first else [logits, hbm(hidden2)]))
-
-
-def policy(logits_raw, labels, acts, batch):
+        compiler_params=params(12 + (8 * width * cut >> 20), "arbitrary"),
+    )(scalars, hidden1, hbm(own), *pieces, theirs, head, *([] if first else [logits, hbm(hidden2)]))
+
+
+def policy(logits_raw, pieces, at, acts, batch):
     total, pad_acts = logits_raw.shape
-
-    def kernel(raw_ref, labels_ref, graw_ref, graw_t_ref, score_ref):
+    count = len(pieces)
+    features = pieces[0].shape[1]
+    per = total // count // features
+    size = pieces[0].shape[0] - at
+
+    def kernel(raw_ref, *refs):
+        label_refs = refs[:count]
+        graw_ref, graw_t_ref, score_ref = refs[count:]
         raw = raw_ref[...].T
-        gains, chosen = labels_ref[0:1, :], labels_ref[1:2, :].astype(jnp.int32)
+        blocks = [ref[...].astype(jnp.float32) for ref in label_refs]
+        part = lambda t: jnp.concatenate(
+            [block[t * per + r : t * per + r + 1, :] for block in blocks for r in range(per)], axis=1
+        )
+        gains, chosen = part(0) + part(1) + part(2), part(3).astype(jnp.int32)
         at = lax.broadcasted_iota(jnp.int32, raw.shape, 0)
         live = at < acts
         squash = jnp.tanh(raw / CAP)
@@ -208,17 +271,24 @@
     return pl.pallas_call(
         kernel,
         name="policy",
+        grid=(1,),
+        in_specs=[whole(logits_raw)] + [pl.BlockSpec((size, features), lambda i: (at // size, 0))] * count,
+        out_specs=[
+            pl.BlockSpec((total, pad_acts), lambda i: (0, 0)),
+            pl.BlockSpec((pad_acts, total), lambda i: (0, 0)),
+            pl.BlockSpec((1, 1), lambda i: (0, 0)),
+        ],
         out_shape=[
             jax.ShapeDtypeStruct((total, pad_acts), jnp.bfloat16),
             jax.ShapeDtypeStruct((pad_acts, total), jnp.bfloat16),
             jax.ShapeDtypeStruct((1, 1), jnp.float32),
         ],
         cost_estimate=cost(1 << 28, 2 << 20),
-        compiler_params=params(10),
-    )(logits_raw, labels)
-
-
-def middle_grad(graw, head, slopes, hidden1_t, first, cut):
+        compiler_params=params(10, "arbitrary"),
+    )(logits_raw, *map(hbm, pieces))
+
+
+def middle_grad(scalars, graw, head, slopes, hidden1_t, start, cut):
     total, pad_acts = graw.shape
     near_rows = hidden1_t.shape[0]
     kept = near_rows // 2
@@ -227,12 +297,13 @@
     parts = len(slopes)
     span = parts * cut
 
-    def kernel(graw_ref, head_ref, *refs):
+    def kernel(scalar_ref, graw_ref, head_ref, *refs):
+        live = scalar_ref[2] == 1
         slope_refs = refs[:parts]
         h1t_ref, g2_ref, keep_ref, give_ref = refs[parts:]
         i = pl.program_id(0)
 
-        @pl.when(i == 0)
+        @pl.when(live & (i == 0))
         def _():
             for p in range(parts):
                 lanes = slice(p * cut, (p + 1) * cut)
@@ -240,22 +311,20 @@
                     g2 = dot(graw_ref[r : r + 256, :], head_ref[:, lanes]) * slope_refs[p][r : r + 256, :].astype(jnp.float32)
                     g2_ref[r : r + 256, lanes] = g2.astype(jnp.bfloat16)
 
-        part = dot(h1t_ref[...], g2_ref[...])
-
-        @pl.when(i < steps // 2)
-        def _():
-            give_ref[...] = part.astype(jnp.bfloat16)
-
-        @pl.when(i >= steps // 2)
-        def _():
-            keep_ref[...] = part
+        @pl.when(live & (i < steps // 2))
+        def _():
+            give_ref[...] = dot(h1t_ref[...], g2_ref[...]).astype(jnp.bfloat16)
+
+        @pl.when(live & (i >= steps // 2))
+        def _():
+            keep_ref[...] = dot(h1t_ref[...], g2_ref[...])
 
     turn = lambda i: (i + steps // 2) % steps
     return pl.pallas_call(
         kernel,
         name="middle_grad",
         grid=(steps,),
-        in_specs=[whole(graw), pl.BlockSpec((pad_acts, span), lambda i: (0, first // parts))]
+        in_specs=[pl.BlockSpec(memory_space=pltpu.SMEM), whole(graw), pl.BlockSpec((pad_acts, span), lambda i: (0, start // span))]
         + [whole(v) for v in slopes]
         + [pl.BlockSpec((tile, total), lambda i: (turn(i), 0))],
         out_specs=[
@@ -264,13 +333,13 @@
             pl.BlockSpec((tile, span), lambda i: (jnp.minimum(i, steps // 2 - 1), 0)),
         ],
         out_shape=[
-            jax.ShapeDtypeStruct((total, span), jnp.bfloat16),
+            pltpu.HBM((total, span), jnp.bfloat16),
             jax.ShapeDtypeStruct((kept, span), jnp.float32),
             pltpu.HBM((kept, span), jnp.bfloat16),
         ],
         cost_estimate=cost(2 * total * near_rows * span, 16 << 20),
         compiler_params=params(24, "arbitrary"),
-    )(graw, head, *slopes, hidden1_t)
+    )(scalars, graw, head, *slopes, hidden1_t)
 
 
 def head_grad(scalars, graw_t, hidden2):
@@ -326,7 +395,7 @@
         out_shape=[pltpu.HBM((slab, span), jnp.bfloat16)] * blocks,
         cost_estimate=cost(1 << 27, 4 << 20),
         compiler_params=params(16, "arbitrary"),
-    )(rate, keep, hbm(got), hbm(own), *map(hbm, flat))
+    )(rate, keep, got, hbm(own), *flat)
 
 
 def gather_small(scalars, order, keep, got, side, score, first_rows, slab, half):
@@ -356,7 +425,7 @@
 
     shape = jax.ShapeDtypeStruct((half, acts_at, slab), jnp.bfloat16)
     smem = pl.BlockSpec(memory_space=pltpu.SMEM)
-    arrays = [keep, hbm(got), side, score]
+    arrays = [keep, got, side, score]
     return pl.pallas_call(
         kernel,
         name="gather_small",
@@ -369,7 +438,7 @@
     )(scalars, order, *arrays)
 
 
-def small_update(scalars, rate, mine, got, weights, score):
+def small_update(scalars, rate, mine, got, weights, score, at_row):
     half, rows, slab = mine.shape
 
     def kernel(scalar_ref, rate_ref, mine_ref, got_ref, *refs):
@@ -384,7 +453,7 @@
         for s in range(half):
             at = jnp.where(high == 1, s, half - 1 - s)
             total = mine_ref[at].astype(jnp.float32) + got_ref[at].astype(jnp.float32)
-            out_refs[s][...] = (weight_refs[s][-rows:, :].astype(jnp.float32) - rate * total).astype(jnp.bfloat16)
+            out_refs[s][...] = (weight_refs[s][at_row : at_row + rows, :].astype(jnp.float32) - rate * total).astype(jnp.bfloat16)
             value = fitness
             for part in range(3):
                 piece = value.astype(jnp.bfloat16)
@@ -401,10 +470,10 @@
         out_shape=[jax.ShapeDtypeStruct((1, 1), jnp.float32)] + [pltpu.HBM((rows, slab), jnp.bfloat16)] * half,
         cost_estimate=cost(1 << 26, 2 << 20),
         compiler_params=params(8, "arbitrary"),
-    )(scalars, rate, mine, hbm(got), *map(hbm, weights), score)
-
-
-def input_grad(scalars, grads, own, near_pieces, theirs, slope, obs_t, cut):
+    )(scalars, rate, mine, got, *map(hbm, weights), score)
+
+
+def input_grad(scalars, grads, own, near_pieces, theirs, slope, obs_t):
     total = grads[0].shape[0]
     slab, width = own.shape
     near_rows = slope.shape[1]
@@ -413,7 +482,9 @@
     groups = len(grads)
     chunks = len(theirs)
     side = features // 2
-    tile = min(256, total)
+    tile = min(512, total)
+    cuts = [v.shape[1] for v in theirs]
+    starts = [sum(cuts[:q]) for q in range(chunks)]
     flat = [p for chunk in near_pieces for p in chunk]
     per = len(flat) // chunks
 
@@ -424,23 +495,26 @@
         theirs_refs, refs = refs[:chunks], refs[chunks:]
         slope_ref, obst_ref, keep_ref, give_ref, weights, total_ref = refs
         i = pl.program_id(0)
-
-        @pl.when(i == 0)
+        live = scalar_ref[2] == 1
+
+        @pl.when(live & (i == 0))
         def _():
             weights[:slab] = own_ref[...]
             for q in range(chunks):
-                lanes = slice(q * cut, (q + 1) * cut)
+                lanes = slice(starts[q], starts[q] + cuts[q])
                 for k in range(per):
                     weights[(k + 1) * slab : (k + 2) * slab, lanes] = flat_refs[q * per + k][...]
                 weights[kept:, lanes] = theirs_refs[q][...]
             total_ref[...] = jnp.zeros_like(total_ref)
 
-        g2 = jnp.concatenate([g[...] for g in g_refs], axis=1)
-        back = dot(g2, weights[...], ((1,), (1,)))
-        grad = (back * slope_ref[...].astype(jnp.float32)).astype(jnp.bfloat16)
-        total_ref[...] += dot(obst_ref[...], grad)
-
-        @pl.when(i == pl.num_programs(0) - 1)
+        @pl.when(live)
+        def _():
+            g2 = jnp.concatenate([g[...] for g in g_refs], axis=1)
+            back = dot(g2, weights[...], ((1,), (1,)))
+            grad = (back * slope_ref[...].astype(jnp.float32)).astype(jnp.bfloat16)
+            total_ref[...] += dot(obst_ref[...], grad)
+
+        @pl.when(live & (i == pl.num_programs(0) - 1))
         def _():
             high = scalar_ref[1]
             keep_ref[...] = total_ref[pl.ds(pl.multiple_of(high * side, side), side), :].astype(jnp.bfloat16)
@@ -454,7 +528,7 @@
         + [pl.BlockSpec((tile, g.shape[1]), lambda i: (i, 0)) for g in grads]
         + [whole(own)]
         + [whole(p) for p in flat]
-        + [pl.BlockSpec((kept, cut), lambda i: (0, 0))] * chunks
+        + [pl.BlockSpec((kept, cut), lambda i: (0, 0)) for cut in cuts]
         + [pl.BlockSpec((tile, near_rows), lambda i: (i, 0)), pl.BlockSpec((features, tile), lambda i: (0, i))],
         out_specs=[pl.BlockSpec((side, near_rows), lambda i: (0, 0))] * 2,
         out_shape=[
@@ -466,8 +540,8 @@
             pltpu.VMEM((features, near_rows), jnp.float32),
         ],
         cost_estimate=cost(2 * total * near_rows * width, 20 << 20),
-        compiler_params=params(26, "arbitrary"),
-    )(scalars, *grads, hbm(own), *map(hbm, flat), *map(hbm, theirs), hbm(slope), hbm(obs_t))
+        compiler_params=params(34, "arbitrary"),
+    )(scalars, *map(hbm, grads), hbm(own), *map(hbm, flat), *map(hbm, theirs), hbm(slope), hbm(obs_t))
 
 
 def settings(numbers, log_rate, copy_from, perturb, devices):
@@ -476,9 +550,9 @@
     def kernel(numbers_ref, log_rate_ref, copy_ref, perturb_ref, order_ref, scalars_ref, rate_ref, flag_ref, next_ref):
         for k in range(devices):
             order_ref[k] = numbers_ref[k]
-        for k in range(2):
+        for k in range(3):
             scalars_ref[k] = numbers_ref[devices + k]
-        member = numbers_ref[devices + 2]
+        member = numbers_ref[devices + 3]
         rate_ref[...] = jnp.exp(jnp.full(rate_ref.shape, log_rate_ref[member], jnp.float32))
         taken = copy_ref[member] == 1
         flag_ref[0] = taken.astype(jnp.int32)
@@ -497,7 +571,7 @@
         out_specs=[smem, smem, vmem, smem, vmem],
         out_shape=[
             ints(devices),
-            ints(2),
+            ints(3),
             jax.ShapeDtypeStruct((8, 128), jnp.float32),
             ints(1),
             jax.ShapeDtypeStruct((1, 1), jnp.float32),
@@ -508,7 +582,7 @@
 
 
 def hub_body(observations, returns, actions, w_input, w_middle, w_head, log_rate, copy_from, perturb):
-    obs, gains, chosen = observations[0], returns[0], actions[0]
+    obs = observations[0]
     own_first, own_middle, own_head = w_input[0], w_middle[0], w_head[0]
     devices = lax.axis_size("dp")
     half = devices // 4
@@ -520,7 +594,9 @@
     pad_acts = -(-(acts + 3) // 32) * 32
     batch = rows * devices
     mids = devices * first_rows
-    cut = width // CHUNKS
+    cuts = [width // part for part in PARTS]
+    starts = [sum(cuts[:q]) for q in range(len(cuts))]
+    cut = min(cuts)
     place = lax.axis_index("dp")
     core = place % 2
     chip = place // 2
@@ -559,7 +635,8 @@
     upper = high ^ ((slots // half) % 2)
     order = 2 * jnp.where(upper == 1, half + slots % half, half - 1 - slots % half) + (core ^ (slots // count))
 
-    numbers = jnp.concatenate([order, jnp.stack([core, high, member])]).astype(jnp.int32)
+    hub = ((chip == half) | (chip == half - 1)).astype(jnp.int32)
+    numbers = jnp.concatenate([order, jnp.stack([core, high, hub, member])]).astype(jnp.int32)
     order, scalars, rate, flag, next_rate = settings(numbers, log_rate, copy_from, perturb, devices)
 
     def column(value):
@@ -570,32 +647,27 @@
             out.append(far(value, s))
         return out
 
-    packed = jnp.concatenate(
-        [
-            obs,
-            own_first.reshape(first_rows, devices, slab).swapaxes(0, 1).reshape(-1, slab),
-            jnp.pad(own_head.T, ((0, pad_acts - acts), (0, 0))),
-        ],
-        axis=0,
-    )
+    labels_at = rows + mids + pad_acts
+    packed = pack(obs, own_first, own_head, returns, actions, slab, pad_acts)
     pieces = [packed] + column(packed)
-    middle_pieces = [column(own_middle[:, q * cut : (q + 1) * cut]) for q in range(CHUNKS)]
-    labels = jnp.stack([gains, chosen.astype(jnp.float32)])
-    labels = jnp.concatenate([labels] + column(labels), axis=1)
-    theirs_small = partner(jnp.stack([p[rows:] for p in pieces]))
-    hidden1, near_t, slope1, obs_t, head = first_layer(order, pieces, theirs_small, rows, slab, half)
+    columns = [own_middle[:, start : start + cut] for start, cut in zip(starts, cuts)]
+    middle_pieces = [column(columns[q]) for q in range(len(cuts))]
+    theirs_small = partner(jnp.stack([p[rows:labels_at] for p in pieces]))
+    hidden1, near_t, slope1, obs_t, head = first_layer(order, scalars, pieces, theirs_small, rows, slab, half, pad_acts)
 
     logits = None
     hidden2, slope2, theirs = None, [], []
-    for q in range(CHUNKS):
-        mine = jnp.concatenate([own_middle[:, q * cut : (q + 1) * cut]] + middle_pieces[q], axis=0)
+    for q in range(len(cuts)):
+        mine = jnp.concatenate([columns[q]] + middle_pieces[q], axis=0)
         theirs.append(partner(mine))
-        hidden2, slope, logits = second_layer(
-            hidden1, own_middle, middle_pieces[q], theirs[q], head, logits, hidden2, q, cut
-        )
-        slope2.append(slope)
-
-    grad_raw, grad_raw_t, score = policy(logits, labels, acts, batch)
+        for inner in range(cuts[q] // cut):
+            start = starts[q] + inner * cut
+            hidden2, slope, logits = second_layer(
+                scalars, hidden1, own_middle, middle_pieces[q], theirs[q], head, logits, hidden2, start, inner, cut
+            )
+            slope2.append(slope)
+
+    grad_raw, grad_raw_t, score = policy(logits, pieces, labels_at, acts, batch)
 
     distance = jnp.where(high == 1, chip - half, half - 1 - chip)
 
@@ -609,26 +681,26 @@
     flag = flag[0] == 1
 
     near_w = [m[: half - 1] for m in middle_pieces]
-    per = CHUNKS // GROUPS
-    span = per * cut
+    span = width // GROUPS
     out_middle, grads = [], []
     for g in range(GROUPS):
-        part = slice(g * per, (g + 1) * per)
-        g2, keep, give = middle_grad(grad_raw, head, slope2[part], near_t, g * per, cut)
+        which = [q for q in range(len(cuts)) if starts[q] // span == g]
+        parts = range(g * span // cut, (g + 1) * span // cut)
+        g2, keep, give = middle_grad(scalars, grad_raw, head, [slope2[p] for p in parts], near_t, g * span, cut)
         got = partner(give)
-        new = middle_update(rate, keep, got, own_middle, near_w[part], g, span, cut)
+        new = middle_update(rate, keep, got, own_middle, [near_w[q] for q in which], g, span, cuts[which[0]])
         new = home(new)
         moved = shifted(new)
         out_middle.append(jnp.where(flag, moved, new))
         grads.append(g2)
     out_middle = jnp.concatenate(out_middle, axis=1)
 
-    keep, give = input_grad(scalars, grads, own_middle, near_w, theirs, slope1, obs_t, cut)
+    keep, give = input_grad(scalars, grads, own_middle, near_w, theirs, slope1, obs_t)
     got = far(give, 0)
     head_term = head_grad(scalars, grad_raw_t, hidden2)
     mine, sent = gather_small(scalars, order, keep, got, head_term, score, first_rows, slab, half)
     got = partner(sent)
-    fitness, *new_small = small_update(scalars, rate, mine, got, pieces[:half], score)
+    fitness, *new_small = small_update(scalars, rate, mine, got, pieces[:half], score, rows)
     new_small = home(new_small)
     fitness = jnp.where(
         distance == 0, fitness, jnp.sum(new_small[-3:, :1].astype(jnp.float32), axis=0, keepdims=True)
@@ -757,6 +829,7 @@
     def step(*arrays):
         observations, w_middle = arrays[0], arrays[4]
         small = observations.shape[1] // 2 <= w_middle.shape[2] and mesh.shape["dp"] % 4 == 0
+        small = small and arrays[3].shape[1] * mesh.shape["dp"] == w_middle.shape[2]
         body = hub_step if small else local
         step = jax.shard_map(body, mesh=mesh, in_specs=in_specs, out_specs=out_specs, check_vma=False)
         return step(*arrays)

time: 253 us -> 229 us (0.905)
  Pallas kernels: 101 us -> 48.3 us
  waiting for transfers between devices: 59.6 us -> 102 us
  starting transfers between devices: 71.5 us -> 56.9 us
  other arithmetic: 4.46 us -> 9.14 us
  local copies, waits for them, and re-layouts: 11.5 us -> 8.5 us
    ppermute x3, waiting for transfers between devices: 21.7 us -> 70.2 us  [outward(): return lax.ppermute(value, 'dp', route(step, False, True))]
    pallas_call x4 -> x2, Pallas kernels: 38.3 us -> 8.56 us  [second_layer(): pl.pallas_call(kernel, name='second_layer', grid=(total // tile,), in_spe...]
    ppermute x13 -> x7, starting transfers between devices: 39.2 us -> 15.5 us  [far(): return lax.ppermute(value, 'dp', route(step, True))]
    ppermute x6 -> x3, starting transfers between devices: 21.7 us -> 32.1 us  [near(): return lax.ppermute(value, 'dp', route(step, False))]
    pallas_call x1, Pallas kernels: 15.8 us -> 7.29 us  [input_grad(): pl.pallas_call(kernel, name='input_grad', grid=(total // tile,), in_specs...]
    pallas_call x1, Pallas kernels: 15 us -> 6.74 us  [first_layer(): pl.pallas_call(kernel, name='first_layer', grid_spec=pltpu.PrefetchScalar...]
    pallas_call x3 -> x4, Pallas kernels: 15.8 us -> 11 us  [the longest x2 7.39 us: middle_grad(): pl.pallas_call(kernel, name='middle_grad', grid=(steps,), in_specs=[pl.Bl...]
    ppermute x6 -> x3, waiting for transfers between devices: 16.1 us -> 11.4 us  [near(): return lax.ppermute(value, 'dp', route(step, False))]
  transfers between devices with their start and end apart: 33 -> 22, of which waited for: 8 -> 8; matrix products, arithmetic and copies ran while one was open for 2% -> 5% of each run, Pallas kernels for 33% -> 15%
where the time goes in v2:
time: 229 us
  waiting for transfers between devices  102 us (45%)
  starting transfers between devices  56.9 us (25%)
  Pallas kernels  48.3 us (21%)
  other arithmetic  9.14 us (4%)
  local copies, waits for them, and re-layouts  8.5 us (4%)
  between operations  4.08 us (2%)
    ppermute x3, waiting for transfers between devices, outward(): return lax.ppermute(value, 'dp', route(step, False, True))  70.2 us
    ppermute x3, starting transfers between devices, near(): return lax.ppermute(value, 'dp', route(step, False))  32.1 us
    ppermute x3, waiting for transfers between devices, shifted(): return lax.ppermute(value, 'pop', ring)  15.9 us
    ppermute x7, starting transfers between devices, far(): return lax.ppermute(value, 'dp', route(step, True))  15.5 us
    ppermute x3, waiting for transfers between devices, near(): return lax.ppermute(value, 'dp', route(step, False))  11.4 us
    pallas_call x2, Pallas kernels, second_layer(): pl.pallas_call(kernel, name='second_layer', grid=(total // tile,), in_spe...  8.56 us
    pallas_call x2, Pallas kernels, middle_grad(): pl.pallas_call(kernel, name='middle_grad', grid=(steps,), in_specs=[pl.Bl...  7.39 us
    pallas_call x1, Pallas kernels, input_grad(): pl.pallas_call(kernel, name='input_grad', grid=(total // tile,), in_specs...  7.29 us
  transfers between devices with their start and end apart: 22, of which 8 were waited for; matrix products, arithmetic and copies ran while one was open for 5% of the time, Pallas kernels for 15%

profile of v2, /device:TPU:0, one launch (start us, length us, event | category | flops | bytes accessed | tf_op | source)
XLA Modules:
  0.0 228.5 jit_solution(17616475162201781043)
XLA Ops:
  2.7 6.0 %collective-permute-start.10 = (bf16[256,1024]{1,0:T(8,128)(2,1)S(1)}, bf16[256,1024]{1,0:T(8,128)(2,1)S(1)}, u32[]{:S(2)}, u32[]{:S(2)}) collective-permute-start(bf16[256,1024]{1,0:T(8,128)(2,1)S(1)} %get-tuple-element.77), channel_id=1, source_target_pairs={{0,4},{1,5},{6,2},{7,3},{8,12},{9,13},{14,10},{15,11},{16,20},{17,... | collective-permute-start | bytes 1572872 | tf_op jit(solution)/shard_map/ppermute | solution.py:623
  9.4 3.1 %collective-permute-start.8 = (bf16[256,1024]{1,0:T(8,128)(2,1)S(1)}, bf16[256,1024]{1,0:T(8,128)(2,1)S(1)}, u32[]{:S(2)}, u32[]{:S(2)}) collective-permute-start(bf16[256,1024]{1,0:T(8,128)(2,1)S(1)} %get-tuple-element.77), channel_id=1, source_target_pairs={{0,2},{1,3},{6,4},{7,5},{8,10},{9,11},{14,12},{15,13},{16,18},{17,... | collective-permute-start | bytes 1572872 | tf_op jit(solution)/shard_map/ppermute | solution.py:620
  18.0 3.0 %collective-permute-done.10.refs_2_ = bf16[256,1024]{1,0:T(8,128)(2,1)S(1)} collective-permute-done((bf16[256,1024]{1,0:T(8,128)(2,1)S(1)}, bf16[256,1024]{1,0:T(8,128)(2,1)S(1)}, u32[]{:S(2)}, u32[]{:S(2)}) %collective-permute-start.10) | collective-permute-done | bytes 524320 | tf_op jit(solution)/shard_map/ppermute | solution.py:623
  21.0 5.3 %collective-permute-start.6 = (bf16[256,1024]{1,0:T(8,128)(2,1)}, bf16[256,1024]{1,0:T(8,128)(2,1)S(1)}, u32[]{:S(2)}, u32[]{:S(2)}) collective-permute-start(bf16[256,1024]{1,0:T(8,128)(2,1)} %get-tuple-element.78), channel_id=1, source_target_pairs={{0,4},{1,5},{6,2},{7,3},{8,12},{9,13},{14,10},{15,11},{16,20},{17,... | collective-permute-start | bytes 1572872 | tf_op jit(solution)/shard_map/ppermute | solution.py:623
  27.0 5.2 %collective-permute-done.8.refs_0_.refs_3_ = bf16[256,1024]{1,0:T(8,128)(2,1)S(1)} collective-permute-done((bf16[256,1024]{1,0:T(8,128)(2,1)S(1)}, bf16[256,1024]{1,0:T(8,128)(2,1)S(1)}, u32[]{:S(2)}, u32[]{:S(2)}) %collective-permute-start.8) | collective-permute-done | bytes 524320 | tf_op jit(solution)/shard_map/ppermute | solution.py:620
  32.2 7.9 %collective-permute-start.4 = (bf16[256,1024]{1,0:T(8,128)(2,1)}, bf16[256,1024]{1,0:T(8,128)(2,1)S(1)}, u32[]{:S(2)}, u32[]{:S(2)}) collective-permute-start(bf16[256,1024]{1,0:T(8,128)(2,1)} %get-tuple-element.78), channel_id=1, source_target_pairs={{0,2},{1,3},{6,4},{7,5},{8,10},{9,11},{14,12},{15,13},{16,18},{17,... | collective-permute-start | bytes 1572872 | tf_op jit(solution)/shard_map/ppermute | solution.py:620
  40.1 2.5 %pad_maximum_fusion.1 = bf16[1024,1024]{1,0:T(8,128)(2,1)} fusion(bf16[256,1024]{1,0:T(8,128)(2,1)S(1)} %collective-permute-done.10.refs_2_, bf16[256,1024]{1,0:T(8,128)(2,1)S(1)} %collective-permute-done.9.refs_1_, bf16[256,1024]{1,0:T(8,128)(2,1)S(1)} %collective-permute-done.8.refs_0_.refs_3_, bf16[256,1024]{1,0:T(8,128)(2,1)} %copy-done.11), kind=kLoop, calls=%fused_computation.1 | loop fusion | flops 8388608 | bytes 4194304 | tf_op jit(solution)/shard_map/concatenate | solution.py:661
  43.5 21.1 %collective-permute-start = (bf16[816,256]{1,0:T(8,128)(2,1)S(1)}, bf16[816,256]{1,0:T(8,128)(2,1)S(1)}, u32[]{:S(2)}, u32[]{:S(2)}) collective-permute-start(bf16[816,256]{1,0:T(8,128)(2,1)S(1)} %copy-done.9), channel_id=1, source_target_pairs={{0,2},{1,3},{6,4},{7,5},{8,10},{9,11},{14,12},{15,13},{16,18},{17,... | collective-permute-start | bytes 1253384 | tf_op jit(solution)/shard_map/ppermute | solution.py:620
  64.7 2.7 %pad_maximum_fusion = bf16[1024,1024]{1,0:T(8,128)(2,1)} fusion(bf16[256,1024]{1,0:T(8,128)(2,1)S(1)} %collective-permute-done.6.refs_2_, bf16[256,1024]{1,0:T(8,128)(2,1)S(1)} %collective-permute-done.5.refs_1_, bf16[256,1024]{1,0:T(8,128)(2,1)S(1)} %collective-permute-done.4.refs_0_.refs_4_, bf16[256,1024]{1,0:T(8,128)(2,1)} %get-tuple-element.78), kind=kLoop, calls=%fused_computation | loop fusion | flops 8388608 | bytes 4194304 | tf_op jit(solution)/shard_map/concatenate | solution.py:661
  67.4 6.2 %collective-permute-done.refs_1_ = bf16[816,256]{1,0:T(8,128)(2,1)S(1)} collective-permute-done((bf16[816,256]{1,0:T(8,128)(2,1)S(1)}, bf16[816,256]{1,0:T(8,128)(2,1)S(1)}, u32[]{:S(2)}, u32[]{:S(2)}) %collective-permute-start) | collective-permute-done | bytes 417824 | tf_op jit(solution)/shard_map/ppermute | solution.py:620
  77.6 6.7 %first_layer.1 = (bf16[2048,2048]{1,0:T(8,128)(2,1)S(1)}, bf16[1024,2048]{1,0:T(8,128)(2,1)S(1)}, bf16[2048,1024]{1,0:T(8,128)(2,1)}, bf16[256,2048]{1,0:T(8,128)(2,1)}, bf16[32,2048]{1,0:T(8,128)(2,1)S(1)}) custom-call(s32[8]{0:T(128)S(1)} %get-tuple-element.44.order_ref, s32[3]{0:T(128)S(1)} %get-tuple-element.42.scalar_ref, ...), custom_call_target="tpu_custom_call" | custom-call | flops 4294967296 | bytes 31457280 | tf_op jit(solution)/shard_map/first_layer/pallas_call | solution.py:156
  84.3 4.3 %second_layer.2 = (bf16[2048,2048]{1,0:T(8,128)(2,1)}, bf16[2048,1024]{1,0:T(8,128)(2,1)S(1)}, f32[2048,32]{1,0:T(8,128)S(1)}) custom-call(s32[3]{0:T(128)S(1)} %get-tuple-element.42.scalar_ref, bf16[2048,2048]{1,0:T(8,128)(2,1)S(1)} %get-tuple-element.45.h1_ref, bf16[256,2048]{1,0:T(8,128)(2,1)} %bitcast.31, ...), custom_call_target="tpu_custom_call" | custom-call | flops 8589934592 | bytes 16777216 | tf_op jit(solution)/shard_map/second_layer/pallas_call | solution.py:220
  90.6 4.3 %second_layer.3 = (bf16[2048,2048]{1,0:T(8,128)(2,1)}, bf16[2048,1024]{1,0:T(8,128)(2,1)S(1)}, f32[2048,32]{1,0:T(8,128)S(1)}) custom-call(s32[3]{0:T(128)S(1)} %get-tuple-element.42.scalar_ref, bf16[2048,2048]{1,0:T(8,128)(2,1)S(1)} %get-tuple-element.45.h1_ref, bf16[256,2048]{1,0:T(8,128)(2,1)} %bitcast.32, ...), custom_call_target="tpu_custom_call", output_to_operand_aliasing={{0}: (9, {})} | custom-call | flops 8589934592 | bytes 16777216 | tf_op jit(solution)/shard_map/second_layer/pallas_call | solution.py:220
  96.6 3.6 %middle_grad.3 = (bf16[2048,1024]{1,0:T(8,128)(2,1)}, f32[512,1024]{1,0:T(8,128)S(1)}, bf16[512,1024]{1,0:T(8,128)(2,1)}) custom-call(s32[3]{0:T(128)S(1)} %get-tuple-element.42.scalar_ref, bf16[2048,32]{1,0:T(8,128)(2,1)S(1)} %get-tuple-element.50.graw_ref, bf16[32,2048]{1,0:T(8,128)(2,1)S(1)} %get-tuple-element.46.refs_4_.head_ref, ...), custom_call_target="tpu_custom_call" | custom-call | flops 4294967296 | bytes 16777216 | tf_op jit(solution)/shard_map/middle_grad/pallas_call | solution.py:323
  100.1 3.8 %middle_grad.2 = (bf16[2048,1024]{1,0:T(8,128)(2,1)}, f32[512,1024]{1,0:T(8,128)S(1)}, bf16[512,1024]{1,0:T(8,128)(2,1)}) custom-call(s32[3]{0:T(128)S(1)} %get-tuple-element.42.scalar_ref, bf16[2048,32]{1,0:T(8,128)(2,1)S(1)} %get-tuple-element.50.graw_ref, bf16[32,2048]{1,0:T(8,128)(2,1)S(1)} %get-tuple-element.46.refs_4_.head_ref, ...), custom_call_target="tpu_custom_call" | custom-call | flops 4294967296 | bytes 16777216 | tf_op jit(solution)/shard_map/middle_grad/pallas_call | solution.py:323
  104.5 7.3 %input_grad.1 = (bf16[128,1024]{1,0:T(8,128)(2,1)S(1)}, bf16[128,1024]{1,0:T(8,128)(2,1)}) custom-call(s32[3]{0:T(128)S(1)} %get-tuple-element.42.scalar_ref, bf16[2048,1024]{1,0:T(8,128)(2,1)} %get-tuple-element.53.refs_0_, bf16[2048,1024]{1,0:T(8,128)(2,1)} %get-tuple-element.55.refs_1_, bf16[256,2048]{1,0:T(8,128)(2,1)} %bitcast.33, ...), custom_call_target="tpu_custom_call" | custom-call | flops 8589934592 | bytes 20971520 | tf_op jit(solution)/shard_map/input_grad/pallas_call | solution.py:523
  112.5 3.3 %head_grad.1.side_ref = f32[32,1024]{1,0:T(8,128)S(1)} custom-call(s32[3]{0:T(128)S(1)} %get-tuple-element.42.scalar_ref, bf16[32,2048]{1,0:T(8,128)(2,1)S(1)} %get-tuple-element.60.graw_t_ref, bf16[2048,2048]{1,0:T(8,128)(2,1)} %get-tuple-element.61.h2_ref), custom_call_target="tpu_custom_call" | custom-call | flops 1073741824 | bytes 6291456 | tf_op jit(solution)/shard_map/head_grad/pallas_call | solution.py:353
  117.9 2.7 %middle_update.3 = (bf16[256,1024]{1,0:T(8,128)(2,1)}, bf16[256,1024]{1,0:T(8,128)(2,1)}) custom-call(f32[8,128]{1,0:T(8,128)S(1)} %get-tuple-element.43.rate_ref, f32[512,1024]{1,0:T(8,128)S(1)} %get-tuple-element.71.keep_ref, bf16[512,1024]{1,0:T(8,128)(2,1)S(1)} %collective-permute-done.19.got_ref, bf16[256,2048]{1,0:T(8,128)(2,1)} %bitcast.34, ...), custom_call_target="tpu_custom_call" | custom-call | flops 134217728 | bytes 4194304 | tf_op jit(solution)/shard_map/middle_update/pallas_call | solution.py:387
  121.9 2.7 %small_update.1 = (f32[1,1]{1,0:T(1,128)}, bf16[288,256]{1,0:T(8,128)(2,1)}, bf16[288,256]{1,0:T(8,128)(2,1)}) custom-call(s32[3]{0:T(128)S(1)} %get-tuple-element.42.scalar_ref, f32[8,128]{1,0:T(8,128)S(1)} %get-tuple-element.43.rate_ref, bf16[2,288,256]{2,1,0:T(8,128)(2,1)S(1)} %get-tuple-element.63.mine_ref, ...), custom_call_target="tpu_custom_call" | custom-call | flops 67108864 | bytes 2097152 | tf_op jit(solution)/shard_map/small_update/pallas_call | solution.py:464
  126.7 3.0 %middle_update.2 = (bf16[256,1024]{1,0:T(8,128)(2,1)}, bf16[256,1024]{1,0:T(8,128)(2,1)}) custom-call(f32[8,128]{1,0:T(8,128)S(1)} %get-tuple-element.43.rate_ref, f32[512,1024]{1,0:T(8,128)S(1)} %get-tuple-element.67.keep_ref, bf16[512,1024]{1,0:T(8,128)(2,1)} %collective-permute-done.16.got_ref, bf16[256,2048]{1,0:T(8,128)(2,1)} %bitcast.35, ...), custom_call_target="tpu_custom_call" | custom-call | flops 134217728 | bytes 4194304 | tf_op jit(solution)/shard_map/middle_update/pallas_call | solution.py:387
  130.9 65.3 %collective-permute-done.14 = bf16[288,256]{1,0:T(8,128)(2,1)S(1)} collective-permute-done((bf16[288,256]{1,0:T(8,128)(2,1)}, bf16[288,256]{1,0:T(8,128)(2,1)S(1)}, u32[]{:S(2)}, u32[]{:S(2)}) %collective-permute-start.14) | collective-permute-done | bytes 147488 | tf_op jit(solution)/shard_map/ppermute | solution.py:626
  202.3 4.9 %collective-permute-done.17 = bf16[256,1024]{1,0:T(8,128)(2,1)S(1)} collective-permute-done((bf16[256,1024]{1,0:T(8,128)(2,1)}, bf16[256,1024]{1,0:T(8,128)(2,1)S(1)}, u32[]{:S(2)}, u32[]{:S(2)}) %collective-permute-start.17) | collective-permute-done | bytes 524320 | tf_op jit(solution)/shard_map/ppermute | solution.py:626
  210.3 6.2 %collective-permute-done.21 = bf16[256,1024]{1,0:T(8,128)(2,1)S(1)} collective-permute-done((bf16[256,1024]{1,0:T(8,128)(2,1)S(1)}, bf16[256,1024]{1,0:T(8,128)(2,1)S(1)}, u32[]{:S(2)}, u32[]{:S(2)}) %collective-permute-start.21) | collective-permute-done | bytes 524320 | tf_op jit(solution)/shard_map/ppermute | solution.py:632
  216.6 9.7 %collective-permute-done.18 = bf16[256,1024]{1,0:T(8,128)(2,1)S(1)} collective-permute-done((bf16[256,1024]{1,0:T(8,128)(2,1)S(1)}, bf16[256,1024]{1,0:T(8,128)(2,1)S(1)}, u32[]{:S(2)}, u32[]{:S(2)}) %collective-permute-start.18) | collective-permute-done | bytes 524320 | tf_op jit(solution)/shard_map/ppermute | solution.py:632
  (91 shorter events, 33.8 us)
Async XLA Ops:
  2.7 18.3 %collective-permute-start.10 = (bf16[256,1024]{1,0:T(8,128)(2,1)S(1)}, bf16[256,1024]{1,0:T(8,128)(2,1)S(1)}, u32[]{:S(2)}, u32[]{:S(2)}) collective-permute-start(bf16[256,1024]{1,0:T(8,128)(2,1)S(1)} %get-tuple-element.77), channel_id=1, source_target_pairs={{0,4},{1,5},{6,2},{7,3},{8,12},{9,13},{14,10},{15,11},{16,20},{17,... | collective-permute-start | bytes 1572872 | tf_op jit(solution)/shard_map/ppermute | solution.py:623
  8.7 17.6 %collective-permute-start.9 = (bf16[256,1024]{1,0:T(8,128)(2,1)S(1)}, bf16[256,1024]{1,0:T(8,128)(2,1)S(1)}, u32[]{:S(2)}, u32[]{:S(2)}) collective-permute-start(bf16[256,1024]{1,0:T(8,128)(2,1)S(1)} %get-tuple-element.77), channel_id=1, source_target_pairs={{2,4},{3,5},{4,2},{5,3},{10,12},{11,13},{12,10},{13,11},{18,20},{1... | collective-permute-start | bytes 1572872 | tf_op jit(solution)/shard_map/ppermute | solution.py:623
  9.4 22.8 %collective-permute-start.8 = (bf16[256,1024]{1,0:T(8,128)(2,1)S(1)}, bf16[256,1024]{1,0:T(8,128)(2,1)S(1)}, u32[]{:S(2)}, u32[]{:S(2)}) collective-permute-start(bf16[256,1024]{1,0:T(8,128)(2,1)S(1)} %get-tuple-element.77), channel_id=1, source_target_pairs={{0,2},{1,3},{6,4},{7,5},{8,10},{9,11},{14,12},{15,13},{16,18},{17,... | collective-permute-start | bytes 1572872 | tf_op jit(solution)/shard_map/ppermute | solution.py:620
  15.8 26.9 %collective-permute-start.2 = (bf16[816,256]{1,0:T(8,128)(2,1)}, bf16[816,256]{1,0:T(8,128)(2,1)S(1)}, u32[]{:S(2)}, u32[]{:S(2)}) collective-permute-start(bf16[816,256]{1,0:T(8,128)(2,1)} %pack.1.refs_0_), channel_id=1, source_target_pairs={{0,4},{1,5},{6,2},{7,3},{8,12},{9,13},{14,10},{15,11},{16,20},{17,... | collective-permute-start | bytes 1253384 | tf_op jit(solution)/shard_map/ppermute | solution.py:623
  17.3 26.2 %collective-permute-start.1 = (bf16[816,256]{1,0:T(8,128)(2,1)}, bf16[816,256]{1,0:T(8,128)(2,1)S(1)}, u32[]{:S(2)}, u32[]{:S(2)}) collective-permute-start(bf16[816,256]{1,0:T(8,128)(2,1)} %pack.1.refs_0_), channel_id=1, source_target_pairs={{2,4},{3,5},{4,2},{5,3},{10,12},{11,13},{12,10},{13,11},{18,20},{1... | collective-permute-start | bytes 1253384 | tf_op jit(solution)/shard_map/ppermute | solution.py:623
  21.0 43.6 %collective-permute-start.6 = (bf16[256,1024]{1,0:T(8,128)(2,1)}, bf16[256,1024]{1,0:T(8,128)(2,1)S(1)}, u32[]{:S(2)}, u32[]{:S(2)}) collective-permute-start(bf16[256,1024]{1,0:T(8,128)(2,1)} %get-tuple-element.78), channel_id=1, source_target_pairs={{0,4},{1,5},{6,2},{7,3},{8,12},{9,13},{14,10},{15,11},{16,20},{17,... | collective-permute-start | bytes 1572872 | tf_op jit(solution)/shard_map/ppermute | solution.py:623
  26.3 38.3 %collective-permute-start.5 = (bf16[256,1024]{1,0:T(8,128)(2,1)}, bf16[256,1024]{1,0:T(8,128)(2,1)S(1)}, u32[]{:S(2)}, u32[]{:S(2)}) collective-permute-start(bf16[256,1024]{1,0:T(8,128)(2,1)} %get-tuple-element.78), channel_id=1, source_target_pairs={{2,4},{3,5},{4,2},{5,3},{10,12},{11,13},{12,10},{13,11},{18,20},{1... | collective-permute-start | bytes 1572872 | tf_op jit(solution)/shard_map/ppermute | solution.py:623
  32.2 32.4 %collective-permute-start.4 = (bf16[256,1024]{1,0:T(8,128)(2,1)}, bf16[256,1024]{1,0:T(8,128)(2,1)S(1)}, u32[]{:S(2)}, u32[]{:S(2)}) collective-permute-start(bf16[256,1024]{1,0:T(8,128)(2,1)} %get-tuple-element.78), channel_id=1, source_target_pairs={{0,2},{1,3},{6,4},{7,5},{8,10},{9,11},{14,12},{15,13},{16,18},{17,... | collective-permute-start | bytes 1572872 | tf_op jit(solution)/shard_map/ppermute | solution.py:620
  42.7 41.6 %collective-permute-start.11 = (bf16[1024,1024]{1,0:T(8,128)(2,1)}, bf16[1024,1024]{1,0:T(8,128)(2,1)}, u32[]{:S(2)}, u32[]{:S(2)}) collective-permute-start(bf16[1024,1024]{1,0:T(8,128)(2,1)} %pad_maximum_fusion.1), channel_id=1, source_target_pairs={{0,1},{1,0},{2,3},{3,2},{4,5},{5,4},{6,7},{7,6},{8,9},{9,8},{10,11... | collective-permute-start | bytes 6291464 | tf_op jit(solution)/shard_map/ppermute | solution.py:629
  43.5 30.1 %collective-permute-start = (bf16[816,256]{1,0:T(8,128)(2,1)S(1)}, bf16[816,256]{1,0:T(8,128)(2,1)S(1)}, u32[]{:S(2)}, u32[]{:S(2)}) collective-permute-start(bf16[816,256]{1,0:T(8,128)(2,1)S(1)} %copy-done.9), channel_id=1, source_target_pairs={{0,2},{1,3},{6,4},{7,5},{8,10},{9,11},{14,12},{15,13},{16,18},{17,... | collective-permute-start | bytes 1253384 | tf_op jit(solution)/shard_map/ppermute | solution.py:620
  67.4 23.2 %collective-permute-start.7 = (bf16[1024,1024]{1,0:T(8,128)(2,1)}, bf16[1024,1024]{1,0:T(8,128)(2,1)}, u32[]{:S(2)}, u32[]{:S(2)}) collective-permute-start(bf16[1024,1024]{1,0:T(8,128)(2,1)} %pad_maximum_fusion), channel_id=1, source_target_pairs={{0,1},{1,0},{2,3},{3,2},{4,5},{5,4},{6,7},{7,6},{8,9},{9,8},{10,11... | collective-permute-start | bytes 6291464 | tf_op jit(solution)/shard_map/ppermute | solution.py:629
  75.2 2.3 %collective-permute-start.3 = (bf16[4,288,256]{2,1,0:T(8,128)(2,1)}, bf16[4,288,256]{2,1,0:T(8,128)(2,1)}, u32[]{:S(2)}, u32[]{:S(2)}) collective-permute-start(bf16[4,288,256]{2,1,0:T(8,128)(2,1)} %pad_maximum_fusion.2), channel_id=1, source_target_pairs={{0,1},{1,0},{2,3},{3,2},{4,5},{5,4},{6,7},{7,6},{8,9},{9,8},{10,11... | collective-permute-start | bytes 1769480 | tf_op jit(solution)/shard_map/ppermute | solution.py:629
  104.0 14.0 %collective-permute-start.19 = (bf16[512,1024]{1,0:T(8,128)(2,1)S(1)}, bf16[512,1024]{1,0:T(8,128)(2,1)S(1)}, u32[]{:S(2)}, u32[]{:S(2)}) collective-permute-start(bf16[512,1024]{1,0:T(8,128)(2,1)S(1)} %copy-done.16), channel_id=1, source_target_pairs={{0,1},{1,0},{2,3},{3,2},{4,5},{5,4},{6,7},{7,6},{8,9},{9,8},{10,11... | collective-permute-start | bytes 3145736 | tf_op jit(solution)/shard_map/ppermute | solution.py:629
  104.1 22.5 %collective-permute-start.16 = (bf16[512,1024]{1,0:T(8,128)(2,1)}, bf16[512,1024]{1,0:T(8,128)(2,1)}, u32[]{:S(2)}, u32[]{:S(2)}) collective-permute-start(bf16[512,1024]{1,0:T(8,128)(2,1)} %get-tuple-element.68), channel_id=1, source_target_pairs={{0,1},{1,0},{2,3},{3,2},{4,5},{5,4},{6,7},{7,6},{8,9},{9,8},{10,11... | collective-permute-start | bytes 3145736 | tf_op jit(solution)/shard_map/ppermute | solution.py:629
  111.8 4.0 %collective-permute-start.12 = (bf16[128,1024]{1,0:T(8,128)(2,1)}, bf16[128,1024]{1,0:T(8,128)(2,1)S(1)}, u32[]{:S(2)}, u32[]{:S(2)}) collective-permute-start(bf16[128,1024]{1,0:T(8,128)(2,1)} %get-tuple-element.59), channel_id=1, source_target_pairs={{2,4},{3,5},{4,2},{5,3},{10,12},{11,13},{12,10},{13,11},{18,20},{1... | collective-permute-start | bytes 786440 | tf_op jit(solution)/shard_map/ppermute | solution.py:623
  117.8 4.1 %collective-permute-start.13 = (bf16[2,288,256]{2,1,0:T(8,128)(2,1)}, bf16[2,288,256]{2,1,0:T(8,128)(2,1)S(1)}, u32[]{:S(2)}, u32[]{:S(2)}) collective-permute-start(bf16[2,288,256]{2,1,0:T(8,128)(2,1)} %get-tuple-element.64), channel_id=1, source_target_pairs={{0,1},{1,0},{2,3},{3,2},{4,5},{5,4},{6,7},{7,6},{8,9},{9,8},{10,11... | collective-permute-start | bytes 884744 | tf_op jit(solution)/shard_map/ppermute | solution.py:629
  120.6 79.1 %collective-permute-start.20 = (bf16[256,1024]{1,0:T(8,128)(2,1)}, bf16[256,1024]{1,0:T(8,128)(2,1)}, u32[]{:S(2)}, u32[]{:S(2)}) collective-permute-start(bf16[256,1024]{1,0:T(8,128)(2,1)} %get-tuple-element.73), channel_id=1, source_target_pairs={{2,0},{3,1},{4,6},{5,7},{10,8},{11,9},{12,14},{13,15},{18,16},{19,... | collective-permute-start | bytes 1572872 | tf_op jit(solution)/shard_map/ppermute | solution.py:626
  124.5 71.7 %copy-start.15 = (bf16[288,256]{1,0:T(8,128)(2,1)S(1)}, bf16[288,256]{1,0:T(8,128)(2,1)}, u32[]{:S(2)}) copy-start(bf16[288,256]{1,0:T(8,128)(2,1)} %get-tuple-element.66) | copy-start | bytes 442372
  124.5 75.1 %copy-start.14 = (bf16[256,1024]{1,0:T(8,128)(2,1)S(1)}, bf16[256,1024]{1,0:T(8,128)(2,1)}, u32[]{:S(2)}) copy-start(bf16[256,1024]{1,0:T(8,128)(2,1)} %get-tuple-element.74) | copy-start | bytes 1572868
  124.5 71.6 %collective-permute-start.14 = (bf16[288,256]{1,0:T(8,128)(2,1)}, bf16[288,256]{1,0:T(8,128)(2,1)S(1)}, u32[]{:S(2)}, u32[]{:S(2)}) collective-permute-start(bf16[288,256]{1,0:T(8,128)(2,1)} %get-tuple-element.65), channel_id=1, source_target_pairs={{2,0},{3,1},{4,6},{5,7},{10,8},{11,9},{12,14},{13,15},{18,16},{19,... | collective-permute-start | bytes 442376 | tf_op jit(solution)/shard_map/ppermute | solution.py:626
  129.6 77.6 %collective-permute-start.17 = (bf16[256,1024]{1,0:T(8,128)(2,1)}, bf16[256,1024]{1,0:T(8,128)(2,1)S(1)}, u32[]{:S(2)}, u32[]{:S(2)}) collective-permute-start(bf16[256,1024]{1,0:T(8,128)(2,1)} %get-tuple-element.69), channel_id=1, source_target_pairs={{2,0},{3,1},{4,6},{5,7},{10,8},{11,9},{12,14},{13,15},{18,16},{19,... | collective-permute-start | bytes 1572872 | tf_op jit(solution)/shard_map/ppermute | solution.py:626
  196.2 12.6 %collective-permute-start.15 = (bf16[288,256]{1,0:T(8,128)(2,1)S(1)}, bf16[288,256]{1,0:T(8,128)(2,1)S(1)}, u32[]{:S(2)}, u32[]{:S(2)}) collective-permute-start(bf16[288,256]{1,0:T(8,128)(2,1)S(1)} %broadcast_select_fusion.4), channel_id=1, source_target_pairs={{0,8},{8,16},{16,24},{24,0},{1,9},{9,17},{17,25},{25,1},{2,10},{10... | collective-permute-start | bytes 442376 | tf_op jit(solution)/shard_map/ppermute | solution.py:632
  200.8 15.7 %collective-permute-start.21 = (bf16[256,1024]{1,0:T(8,128)(2,1)S(1)}, bf16[256,1024]{1,0:T(8,128)(2,1)S(1)}, u32[]{:S(2)}, u32[]{:S(2)}) collective-permute-start(bf16[256,1024]{1,0:T(8,128)(2,1)S(1)} %broadcast_select_fusion), channel_id=1, source_target_pairs={{0,8},{8,16},{16,24},{24,0},{1,9},{9,17},{17,25},{25,1},{2,10},{10... | collective-permute-start | bytes 1572872 | tf_op jit(solution)/shard_map/ppermute | solution.py:632
  207.3 19.0 %collective-permute-start.18 = (bf16[256,1024]{1,0:T(8,128)(2,1)S(1)}, bf16[256,1024]{1,0:T(8,128)(2,1)S(1)}, u32[]{:S(2)}, u32[]{:S(2)}) collective-permute-start(bf16[256,1024]{1,0:T(8,128)(2,1)S(1)} %broadcast_select_fusion.1), channel_id=1, source_target_pairs={{0,8},{8,16},{16,24},{24,0},{1,9},{9,17},{17,25},{25,1},{2,10},{10... | collective-permute-start | bytes 1572872 | tf_op jit(solution)/shard_map/ppermute | solution.py:632
  (15 other events, 285.5 us)

commit v3 on v2

--- a/solution.py
+++ b/solution.py
@@ -55,7 +55,7 @@
     rows, features = obs.shape
     each, width = first.shape
     devices = width // slab
-    acts = head.shape[1]
+    acts = head.shape[0]
     mids = devices * each
     per = rows // features
     at = rows + mids + pad_acts
@@ -65,10 +65,8 @@
         out_ref[:rows, :] = obs_ref[...]
         for b in range(devices):
             out_ref[rows + b * each : rows + (b + 1) * each, :] = first_ref[:, b * slab : (b + 1) * slab]
-        block = head_ref[...].astype(jnp.float32)
-        block = jnp.concatenate([block, jnp.zeros((slab, 128 - acts), jnp.float32)], axis=1)
-        out_ref[rows + mids : at, :] = block.T[:pad_acts].astype(jnp.bfloat16)
-        out_ref[at:, :] = jnp.zeros((total - at, features), jnp.bfloat16)
+        out_ref[rows + mids :, :] = jnp.zeros((total - rows - mids, features), jnp.bfloat16)
+        out_ref[rows + mids : rows + mids + acts, :] = head_ref[...]
         value = gains_ref[...]
         parts = []
         for _ in range(3):
@@ -648,7 +646,7 @@
         return out
 
     labels_at = rows + mids + pad_acts
-    packed = pack(obs, own_first, own_head, returns, actions, slab, pad_acts)
+    packed = pack(obs, own_first, own_head.T, returns, actions, slab, pad_acts)
     pieces = [packed] + column(packed)
     columns = [own_middle[:, start : start + cut] for start, cut in zip(starts, cuts)]
     middle_pieces = [column(columns[q]) for q in range(len(cuts))]

time: 229 us -> 227 us (level)
    unnamed x35 -> x32, local copies, waits for them, and re-layouts: 4.89 us -> 3.42 us
  transfers between devices with their start and end apart: 22 -> 22, of which waited for: 8 -> 8; matrix products, arithmetic and copies ran while one was open for 5% -> 3% of each run, Pallas kernels for 15% -> 15%
where the time goes in v3:
time: 227 us
  waiting for transfers between devices  103 us (45%)
  starting transfers between devices  57.9 us (26%)
  Pallas kernels  48.4 us (21%)
  other arithmetic  6.87 us (3%)
  local copies, waits for them, and re-layouts  6.24 us (3%)
  between operations  4.13 us (2%)
    ppermute x3, waiting for transfers between devices, outward(): return lax.ppermute(value, 'dp', route(step, False, True))  68.9 us
    ppermute x3, starting transfers between devices, near(): return lax.ppermute(value, 'dp', route(step, False))  33.1 us
    ppermute x3, waiting for transfers between devices, shifted(): return lax.ppermute(value, 'pop', ring)  16 us
    ppermute x7, starting transfers between devices, far(): return lax.ppermute(value, 'dp', route(step, True))  15.5 us
    ppermute x3, waiting for transfers between devices, near(): return lax.ppermute(value, 'dp', route(step, False))  12.6 us
    pallas_call x2, Pallas kernels, second_layer(): pl.pallas_call(kernel, name='second_layer', grid=(total // tile,), in_spe...  8.57 us
    pallas_call x2, Pallas kernels, middle_grad(): pl.pallas_call(kernel, name='middle_grad', grid=(steps,), in_specs=[pl.Bl...  7.44 us
    pallas_call x1, Pallas kernels, input_grad(): pl.pallas_call(kernel, name='input_grad', grid=(total // tile,), in_specs...  7.29 us
  transfers between devices with their start and end apart: 22, of which 8 were waited for; matrix products, arithmetic and copies ran while one was open for 3% of the time, Pallas kernels for 15%

profile of v3, /device:TPU:0, one launch (start us, length us, event | category | flops | bytes accessed | tf_op | source)
XLA Modules:
  0.0 226.6 jit_solution(9338561549324371258)
XLA Ops:
  1.9 6.0 %collective-permute-start.10 = (bf16[256,1024]{1,0:T(8,128)(2,1)S(1)}, bf16[256,1024]{1,0:T(8,128)(2,1)S(1)}, u32[]{:S(2)}, u32[]{:S(2)}) collective-permute-start(bf16[256,1024]{1,0:T(8,128)(2,1)S(1)} %get-tuple-element.77), channel_id=1, source_target_pairs={{0,4},{1,5},{6,2},{7,3},{8,12},{9,13},{14,10},{15,11},{16,20},{17,... | collective-permute-start | bytes 1572872 | tf_op jit(solution)/shard_map/ppermute | solution.py:621
  8.6 3.1 %collective-permute-start.8 = (bf16[256,1024]{1,0:T(8,128)(2,1)S(1)}, bf16[256,1024]{1,0:T(8,128)(2,1)S(1)}, u32[]{:S(2)}, u32[]{:S(2)}) collective-permute-start(bf16[256,1024]{1,0:T(8,128)(2,1)S(1)} %get-tuple-element.77), channel_id=1, source_target_pairs={{0,2},{1,3},{6,4},{7,5},{8,10},{9,11},{14,12},{15,13},{16,18},{17,... | collective-permute-start | bytes 1572872 | tf_op jit(solution)/shard_map/ppermute | solution.py:618
  15.7 4.5 %collective-permute-done.10.refs_2_ = bf16[256,1024]{1,0:T(8,128)(2,1)S(1)} collective-permute-done((bf16[256,1024]{1,0:T(8,128)(2,1)S(1)}, bf16[256,1024]{1,0:T(8,128)(2,1)S(1)}, u32[]{:S(2)}, u32[]{:S(2)}) %collective-permute-start.10) | collective-permute-done | bytes 524320 | tf_op jit(solution)/shard_map/ppermute | solution.py:621
  20.2 5.3 %collective-permute-start.6 = (bf16[256,1024]{1,0:T(8,128)(2,1)S(1)}, bf16[256,1024]{1,0:T(8,128)(2,1)S(1)}, u32[]{:S(2)}, u32[]{:S(2)}) collective-permute-start(bf16[256,1024]{1,0:T(8,128)(2,1)S(1)} %get-tuple-element.78), channel_id=1, source_target_pairs={{0,4},{1,5},{6,2},{7,3},{8,12},{9,13},{14,10},{15,11},{16,20},{17,... | collective-permute-start | bytes 1572872 | tf_op jit(solution)/shard_map/ppermute | solution.py:621
  26.2 5.2 %collective-permute-done.8.refs_0_.refs_3_ = bf16[256,1024]{1,0:T(8,128)(2,1)S(1)} collective-permute-done((bf16[256,1024]{1,0:T(8,128)(2,1)S(1)}, bf16[256,1024]{1,0:T(8,128)(2,1)S(1)}, u32[]{:S(2)}, u32[]{:S(2)}) %collective-permute-start.8) | collective-permute-done | bytes 524320 | tf_op jit(solution)/shard_map/ppermute | solution.py:618
  31.5 7.9 %collective-permute-start.4 = (bf16[256,1024]{1,0:T(8,128)(2,1)S(1)}, bf16[256,1024]{1,0:T(8,128)(2,1)S(1)}, u32[]{:S(2)}, u32[]{:S(2)}) collective-permute-start(bf16[256,1024]{1,0:T(8,128)(2,1)S(1)} %get-tuple-element.78), channel_id=1, source_target_pairs={{0,2},{1,3},{6,4},{7,5},{8,10},{9,11},{14,12},{15,13},{16,18},{17,... | collective-permute-start | bytes 1572872 | tf_op jit(solution)/shard_map/ppermute | solution.py:618
  41.6 22.2 %collective-permute-start = (bf16[816,256]{1,0:T(8,128)(2,1)S(1)}, bf16[816,256]{1,0:T(8,128)(2,1)S(1)}, u32[]{:S(2)}, u32[]{:S(2)}) collective-permute-start(bf16[816,256]{1,0:T(8,128)(2,1)S(1)} %copy-done.9), channel_id=1, source_target_pairs={{0,2},{1,3},{6,4},{7,5},{8,10},{9,11},{14,12},{15,13},{16,18},{17,... | collective-permute-start | bytes 1253384 | tf_op jit(solution)/shard_map/ppermute | solution.py:618
  65.4 7.4 %collective-permute-done.refs_1_ = bf16[816,256]{1,0:T(8,128)(2,1)S(1)} collective-permute-done((bf16[816,256]{1,0:T(8,128)(2,1)S(1)}, bf16[816,256]{1,0:T(8,128)(2,1)S(1)}, u32[]{:S(2)}, u32[]{:S(2)}) %collective-permute-start) | collective-permute-done | bytes 417824 | tf_op jit(solution)/shard_map/ppermute | solution.py:618
  76.8 6.7 %first_layer.1 = (bf16[2048,2048]{1,0:T(8,128)(2,1)S(1)}, bf16[1024,2048]{1,0:T(8,128)(2,1)S(1)}, bf16[2048,1024]{1,0:T(8,128)(2,1)}, bf16[256,2048]{1,0:T(8,128)(2,1)}, bf16[32,2048]{1,0:T(8,128)(2,1)S(1)}) custom-call(s32[8]{0:T(128)S(1)} %get-tuple-element.44.order_ref, s32[3]{0:T(128)S(1)} %get-tuple-element.42.scalar_ref, ...), custom_call_target="tpu_custom_call" | custom-call | flops 4294967296 | bytes 31457280 | tf_op jit(solution)/shard_map/first_layer/pallas_call | solution.py:154
  83.5 4.2 %second_layer.2 = (bf16[2048,2048]{1,0:T(8,128)(2,1)}, bf16[2048,1024]{1,0:T(8,128)(2,1)S(1)}, f32[2048,32]{1,0:T(8,128)S(1)}) custom-call(s32[3]{0:T(128)S(1)} %get-tuple-element.42.scalar_ref, bf16[2048,2048]{1,0:T(8,128)(2,1)S(1)} %get-tuple-element.45.h1_ref, bf16[256,2048]{1,0:T(8,128)(2,1)} %bitcast.33, ...), custom_call_target="tpu_custom_call" | custom-call | flops 8589934592 | bytes 16777216 | tf_op jit(solution)/shard_map/second_layer/pallas_call | solution.py:218
  87.8 2.0 copy-done.7
  89.8 4.3 %second_layer.3 = (bf16[2048,2048]{1,0:T(8,128)(2,1)}, bf16[2048,1024]{1,0:T(8,128)(2,1)S(1)}, f32[2048,32]{1,0:T(8,128)S(1)}) custom-call(s32[3]{0:T(128)S(1)} %get-tuple-element.42.scalar_ref, bf16[2048,2048]{1,0:T(8,128)(2,1)S(1)} %get-tuple-element.45.h1_ref, bf16[256,2048]{1,0:T(8,128)(2,1)} %bitcast.34, ...), custom_call_target="tpu_custom_call", output_to_operand_aliasing={{0}: (9, {})} | custom-call | flops 8589934592 | bytes 16777216 | tf_op jit(solution)/shard_map/second_layer/pallas_call | solution.py:218
  95.8 3.6 %middle_grad.3 = (bf16[2048,1024]{1,0:T(8,128)(2,1)}, f32[512,1024]{1,0:T(8,128)S(1)}, bf16[512,1024]{1,0:T(8,128)(2,1)}) custom-call(s32[3]{0:T(128)S(1)} %get-tuple-element.42.scalar_ref, bf16[2048,32]{1,0:T(8,128)(2,1)S(1)} %get-tuple-element.50.graw_ref, bf16[32,2048]{1,0:T(8,128)(2,1)S(1)} %get-tuple-element.46.refs_4_.head_ref, ...), custom_call_target="tpu_custom_call" | custom-call | flops 4294967296 | bytes 16777216 | tf_op jit(solution)/shard_map/middle_grad/pallas_call | solution.py:321
  99.4 3.8 %middle_grad.2 = (bf16[2048,1024]{1,0:T(8,128)(2,1)}, f32[512,1024]{1,0:T(8,128)S(1)}, bf16[512,1024]{1,0:T(8,128)(2,1)}) custom-call(s32[3]{0:T(128)S(1)} %get-tuple-element.42.scalar_ref, bf16[2048,32]{1,0:T(8,128)(2,1)S(1)} %get-tuple-element.50.graw_ref, bf16[32,2048]{1,0:T(8,128)(2,1)S(1)} %get-tuple-element.46.refs_4_.head_ref, ...), custom_call_target="tpu_custom_call" | custom-call | flops 4294967296 | bytes 16777216 | tf_op jit(solution)/shard_map/middle_grad/pallas_call | solution.py:321
  103.8 7.3 %input_grad.1 = (bf16[128,1024]{1,0:T(8,128)(2,1)S(1)}, bf16[128,1024]{1,0:T(8,128)(2,1)}) custom-call(s32[3]{0:T(128)S(1)} %get-tuple-element.42.scalar_ref, bf16[2048,1024]{1,0:T(8,128)(2,1)} %get-tuple-element.53.refs_0_, bf16[2048,1024]{1,0:T(8,128)(2,1)} %get-tuple-element.55.refs_1_, bf16[256,2048]{1,0:T(8,128)(2,1)} %bitcast.35, ...), custom_call_target="tpu_custom_call" | custom-call | flops 8589934592 | bytes 20971520 | tf_op jit(solution)/shard_map/input_grad/pallas_call | solution.py:521
  111.7 3.3 %head_grad.1.side_ref = f32[32,1024]{1,0:T(8,128)S(1)} custom-call(s32[3]{0:T(128)S(1)} %get-tuple-element.42.scalar_ref, bf16[32,2048]{1,0:T(8,128)(2,1)S(1)} %get-tuple-element.60.graw_t_ref, bf16[2048,2048]{1,0:T(8,128)(2,1)} %get-tuple-element.61.h2_ref), custom_call_target="tpu_custom_call" | custom-call | flops 1073741824 | bytes 6291456 | tf_op jit(solution)/shard_map/head_grad/pallas_call | solution.py:351
  115.0 2.0 gather_small.1
  117.2 2.7 %middle_update.3 = (bf16[256,1024]{1,0:T(8,128)(2,1)}, bf16[256,1024]{1,0:T(8,128)(2,1)}) custom-call(f32[8,128]{1,0:T(8,128)S(1)} %get-tuple-element.43.rate_ref, f32[512,1024]{1,0:T(8,128)S(1)} %get-tuple-element.71.keep_ref, bf16[512,1024]{1,0:T(8,128)(2,1)S(1)} %collective-permute-done.19.got_ref, bf16[256,2048]{1,0:T(8,128)(2,1)} %bitcast.36, ...), custom_call_target="tpu_custom_call" | custom-call | flops 134217728 | bytes 4194304 | tf_op jit(solution)/shard_map/middle_update/pallas_call | solution.py:385
  121.2 2.7 %small_update.1 = (f32[1,1]{1,0:T(1,128)}, bf16[288,256]{1,0:T(8,128)(2,1)}, bf16[288,256]{1,0:T(8,128)(2,1)}) custom-call(s32[3]{0:T(128)S(1)} %get-tuple-element.42.scalar_ref, f32[8,128]{1,0:T(8,128)S(1)} %get-tuple-element.43.rate_ref, bf16[2,288,256]{2,1,0:T(8,128)(2,1)S(1)} %get-tuple-element.63.mine_ref, ...), custom_call_target="tpu_custom_call" | custom-call | flops 67108864 | bytes 2097152 | tf_op jit(solution)/shard_map/small_update/pallas_call | solution.py:462
  125.9 3.0 %middle_update.2 = (bf16[256,1024]{1,0:T(8,128)(2,1)}, bf16[256,1024]{1,0:T(8,128)(2,1)}) custom-call(f32[8,128]{1,0:T(8,128)S(1)} %get-tuple-element.43.rate_ref, f32[512,1024]{1,0:T(8,128)S(1)} %get-tuple-element.67.keep_ref, bf16[512,1024]{1,0:T(8,128)(2,1)} %collective-permute-done.16.got_ref, bf16[256,2048]{1,0:T(8,128)(2,1)} %bitcast.37, ...), custom_call_target="tpu_custom_call" | custom-call | flops 134217728 | bytes 4194304 | tf_op jit(solution)/shard_map/middle_update/pallas_call | solution.py:385
  130.2 64.0 %collective-permute-done.14 = bf16[288,256]{1,0:T(8,128)(2,1)S(1)} collective-permute-done((bf16[288,256]{1,0:T(8,128)(2,1)}, bf16[288,256]{1,0:T(8,128)(2,1)S(1)}, u32[]{:S(2)}, u32[]{:S(2)}) %collective-permute-start.14) | collective-permute-done | bytes 147488 | tf_op jit(solution)/shard_map/ppermute | solution.py:624
  200.4 4.9 %collective-permute-done.17 = bf16[256,1024]{1,0:T(8,128)(2,1)S(1)} collective-permute-done((bf16[256,1024]{1,0:T(8,128)(2,1)}, bf16[256,1024]{1,0:T(8,128)(2,1)S(1)}, u32[]{:S(2)}, u32[]{:S(2)}) %collective-permute-start.17) | collective-permute-done | bytes 524320 | tf_op jit(solution)/shard_map/ppermute | solution.py:624
  208.3 6.3 %collective-permute-done.21 = bf16[256,1024]{1,0:T(8,128)(2,1)S(1)} collective-permute-done((bf16[256,1024]{1,0:T(8,128)(2,1)S(1)}, bf16[256,1024]{1,0:T(8,128)(2,1)S(1)}, u32[]{:S(2)}, u32[]{:S(2)}) %collective-permute-start.21) | collective-permute-done | bytes 524320 | tf_op jit(solution)/shard_map/ppermute | solution.py:630
  214.7 9.7 %collective-permute-done.18 = bf16[256,1024]{1,0:T(8,128)(2,1)S(1)} collective-permute-done((bf16[256,1024]{1,0:T(8,128)(2,1)S(1)}, bf16[256,1024]{1,0:T(8,128)(2,1)S(1)}, u32[]{:S(2)}, u32[]{:S(2)}) %collective-permute-start.18) | collective-permute-done | bytes 524320 | tf_op jit(solution)/shard_map/ppermute | solution.py:630
  (88 shorter events, 30.5 us)
Async XLA Ops:
  1.9 18.3 %collective-permute-start.10 = (bf16[256,1024]{1,0:T(8,128)(2,1)S(1)}, bf16[256,1024]{1,0:T(8,128)(2,1)S(1)}, u32[]{:S(2)}, u32[]{:S(2)}) collective-permute-start(bf16[256,1024]{1,0:T(8,128)(2,1)S(1)} %get-tuple-element.77), channel_id=1, source_target_pairs={{0,4},{1,5},{6,2},{7,3},{8,12},{9,13},{14,10},{15,11},{16,20},{17,... | collective-permute-start | bytes 1572872 | tf_op jit(solution)/shard_map/ppermute | solution.py:621
  7.9 17.6 %collective-permute-start.9 = (bf16[256,1024]{1,0:T(8,128)(2,1)S(1)}, bf16[256,1024]{1,0:T(8,128)(2,1)S(1)}, u32[]{:S(2)}, u32[]{:S(2)}) collective-permute-start(bf16[256,1024]{1,0:T(8,128)(2,1)S(1)} %get-tuple-element.77), channel_id=1, source_target_pairs={{2,4},{3,5},{4,2},{5,3},{10,12},{11,13},{12,10},{13,11},{18,20},{1... | collective-permute-start | bytes 1572872 | tf_op jit(solution)/shard_map/ppermute | solution.py:621
  8.6 22.8 %collective-permute-start.8 = (bf16[256,1024]{1,0:T(8,128)(2,1)S(1)}, bf16[256,1024]{1,0:T(8,128)(2,1)S(1)}, u32[]{:S(2)}, u32[]{:S(2)}) collective-permute-start(bf16[256,1024]{1,0:T(8,128)(2,1)S(1)} %get-tuple-element.77), channel_id=1, source_target_pairs={{0,2},{1,3},{6,4},{7,5},{8,10},{9,11},{14,12},{15,13},{16,18},{17,... | collective-permute-start | bytes 1572872 | tf_op jit(solution)/shard_map/ppermute | solution.py:618
  13.6 27.3 %collective-permute-start.2 = (bf16[816,256]{1,0:T(8,128)(2,1)}, bf16[816,256]{1,0:T(8,128)(2,1)S(1)}, u32[]{:S(2)}, u32[]{:S(2)}) collective-permute-start(bf16[816,256]{1,0:T(8,128)(2,1)} %pack.1.refs_0_), channel_id=1, source_target_pairs={{0,4},{1,5},{6,2},{7,3},{8,12},{9,13},{14,10},{15,11},{16,20},{17,... | collective-permute-start | bytes 1253384 | tf_op jit(solution)/shard_map/ppermute | solution.py:621
  15.0 26.6 %collective-permute-start.1 = (bf16[816,256]{1,0:T(8,128)(2,1)}, bf16[816,256]{1,0:T(8,128)(2,1)S(1)}, u32[]{:S(2)}, u32[]{:S(2)}) collective-permute-start(bf16[816,256]{1,0:T(8,128)(2,1)} %pack.1.refs_0_), channel_id=1, source_target_pairs={{2,4},{3,5},{4,2},{5,3},{10,12},{11,13},{12,10},{13,11},{18,20},{1... | collective-permute-start | bytes 1253384 | tf_op jit(solution)/shard_map/ppermute | solution.py:621
  20.2 43.6 %collective-permute-start.6 = (bf16[256,1024]{1,0:T(8,128)(2,1)S(1)}, bf16[256,1024]{1,0:T(8,128)(2,1)S(1)}, u32[]{:S(2)}, u32[]{:S(2)}) collective-permute-start(bf16[256,1024]{1,0:T(8,128)(2,1)S(1)} %get-tuple-element.78), channel_id=1, source_target_pairs={{0,4},{1,5},{6,2},{7,3},{8,12},{9,13},{14,10},{15,11},{16,20},{17,... | collective-permute-start | bytes 1572872 | tf_op jit(solution)/shard_map/ppermute | solution.py:621
  25.5 38.3 %collective-permute-start.5 = (bf16[256,1024]{1,0:T(8,128)(2,1)S(1)}, bf16[256,1024]{1,0:T(8,128)(2,1)S(1)}, u32[]{:S(2)}, u32[]{:S(2)}) collective-permute-start(bf16[256,1024]{1,0:T(8,128)(2,1)S(1)} %get-tuple-element.78), channel_id=1, source_target_pairs={{2,4},{3,5},{4,2},{5,3},{10,12},{11,13},{12,10},{13,11},{18,20},{1... | collective-permute-start | bytes 1572872 | tf_op jit(solution)/shard_map/ppermute | solution.py:621
  31.5 32.4 %collective-permute-start.4 = (bf16[256,1024]{1,0:T(8,128)(2,1)S(1)}, bf16[256,1024]{1,0:T(8,128)(2,1)S(1)}, u32[]{:S(2)}, u32[]{:S(2)}) collective-permute-start(bf16[256,1024]{1,0:T(8,128)(2,1)S(1)} %get-tuple-element.78), channel_id=1, source_target_pairs={{0,2},{1,3},{6,4},{7,5},{8,10},{9,11},{14,12},{15,13},{16,18},{17,... | collective-permute-start | bytes 1572872 | tf_op jit(solution)/shard_map/ppermute | solution.py:618
  40.9 42.7 %collective-permute-start.11 = (bf16[1024,1024]{1,0:T(8,128)(2,1)}, bf16[1024,1024]{1,0:T(8,128)(2,1)}, u32[]{:S(2)}, u32[]{:S(2)}) collective-permute-start(bf16[1024,1024]{1,0:T(8,128)(2,1)} %pad_maximum_fusion.1), channel_id=1, source_target_pairs={{0,1},{1,0},{2,3},{3,2},{4,5},{5,4},{6,7},{7,6},{8,9},{9,8},{10,11... | collective-permute-start | bytes 6291464 | tf_op jit(solution)/shard_map/ppermute | solution.py:627
  41.6 31.1 %collective-permute-start = (bf16[816,256]{1,0:T(8,128)(2,1)S(1)}, bf16[816,256]{1,0:T(8,128)(2,1)S(1)}, u32[]{:S(2)}, u32[]{:S(2)}) collective-permute-start(bf16[816,256]{1,0:T(8,128)(2,1)S(1)} %copy-done.9), channel_id=1, source_target_pairs={{0,2},{1,3},{6,4},{7,5},{8,10},{9,11},{14,12},{15,13},{16,18},{17,... | collective-permute-start | bytes 1253384 | tf_op jit(solution)/shard_map/ppermute | solution.py:618
  65.4 24.4 %collective-permute-start.7 = (bf16[1024,1024]{1,0:T(8,128)(2,1)}, bf16[1024,1024]{1,0:T(8,128)(2,1)}, u32[]{:S(2)}, u32[]{:S(2)}) collective-permute-start(bf16[1024,1024]{1,0:T(8,128)(2,1)} %pad_maximum_fusion), channel_id=1, source_target_pairs={{0,1},{1,0},{2,3},{3,2},{4,5},{5,4},{6,7},{7,6},{8,9},{9,8},{10,11... | collective-permute-start | bytes 6291464 | tf_op jit(solution)/shard_map/ppermute | solution.py:627
  74.4 2.3 %collective-permute-start.3 = (bf16[4,288,256]{2,1,0:T(8,128)(2,1)}, bf16[4,288,256]{2,1,0:T(8,128)(2,1)}, u32[]{:S(2)}, u32[]{:S(2)}) collective-permute-start(bf16[4,288,256]{2,1,0:T(8,128)(2,1)} %pad_maximum_fusion.2), channel_id=1, source_target_pairs={{0,1},{1,0},{2,3},{3,2},{4,5},{5,4},{6,7},{7,6},{8,9},{9,8},{10,11... | collective-permute-start | bytes 1769480 | tf_op jit(solution)/shard_map/ppermute | solution.py:627
  103.3 13.9 %collective-permute-start.19 = (bf16[512,1024]{1,0:T(8,128)(2,1)S(1)}, bf16[512,1024]{1,0:T(8,128)(2,1)S(1)}, u32[]{:S(2)}, u32[]{:S(2)}) collective-permute-start(bf16[512,1024]{1,0:T(8,128)(2,1)S(1)} %copy-done.15), channel_id=1, source_target_pairs={{0,1},{1,0},{2,3},{3,2},{4,5},{5,4},{6,7},{7,6},{8,9},{9,8},{10,11... | collective-permute-start | bytes 3145736 | tf_op jit(solution)/shard_map/ppermute | solution.py:627
  103.4 22.5 %collective-permute-start.16 = (bf16[512,1024]{1,0:T(8,128)(2,1)}, bf16[512,1024]{1,0:T(8,128)(2,1)}, u32[]{:S(2)}, u32[]{:S(2)}) collective-permute-start(bf16[512,1024]{1,0:T(8,128)(2,1)} %get-tuple-element.68), channel_id=1, source_target_pairs={{0,1},{1,0},{2,3},{3,2},{4,5},{5,4},{6,7},{7,6},{8,9},{9,8},{10,11... | collective-permute-start | bytes 3145736 | tf_op jit(solution)/shard_map/ppermute | solution.py:627
  111.1 4.0 %collective-permute-start.12 = (bf16[128,1024]{1,0:T(8,128)(2,1)}, bf16[128,1024]{1,0:T(8,128)(2,1)S(1)}, u32[]{:S(2)}, u32[]{:S(2)}) collective-permute-start(bf16[128,1024]{1,0:T(8,128)(2,1)} %get-tuple-element.59), channel_id=1, source_target_pairs={{2,4},{3,5},{4,2},{5,3},{10,12},{11,13},{12,10},{13,11},{18,20},{1... | collective-permute-start | bytes 786440 | tf_op jit(solution)/shard_map/ppermute | solution.py:621
  117.1 4.1 %collective-permute-start.13 = (bf16[2,288,256]{2,1,0:T(8,128)(2,1)}, bf16[2,288,256]{2,1,0:T(8,128)(2,1)S(1)}, u32[]{:S(2)}, u32[]{:S(2)}) collective-permute-start(bf16[2,288,256]{2,1,0:T(8,128)(2,1)} %get-tuple-element.64), channel_id=1, source_target_pairs={{0,1},{1,0},{2,3},{3,2},{4,5},{5,4},{6,7},{7,6},{8,9},{9,8},{10,11... | collective-permute-start | bytes 884744 | tf_op jit(solution)/shard_map/ppermute | solution.py:627
  119.9 77.9 %collective-permute-start.20 = (bf16[256,1024]{1,0:T(8,128)(2,1)}, bf16[256,1024]{1,0:T(8,128)(2,1)}, u32[]{:S(2)}, u32[]{:S(2)}) collective-permute-start(bf16[256,1024]{1,0:T(8,128)(2,1)} %get-tuple-element.73), channel_id=1, source_target_pairs={{2,0},{3,1},{4,6},{5,7},{10,8},{11,9},{12,14},{13,15},{18,16},{19,... | collective-permute-start | bytes 1572872 | tf_op jit(solution)/shard_map/ppermute | solution.py:624
  123.8 70.4 %copy-start.14 = (bf16[288,256]{1,0:T(8,128)(2,1)S(1)}, bf16[288,256]{1,0:T(8,128)(2,1)}, u32[]{:S(2)}) copy-start(bf16[288,256]{1,0:T(8,128)(2,1)} %get-tuple-element.66) | copy-start | bytes 442372
  123.8 73.9 %copy-start.13 = (bf16[256,1024]{1,0:T(8,128)(2,1)S(1)}, bf16[256,1024]{1,0:T(8,128)(2,1)}, u32[]{:S(2)}) copy-start(bf16[256,1024]{1,0:T(8,128)(2,1)} %get-tuple-element.74) | copy-start | bytes 1572868
  123.8 70.4 %collective-permute-start.14 = (bf16[288,256]{1,0:T(8,128)(2,1)}, bf16[288,256]{1,0:T(8,128)(2,1)S(1)}, u32[]{:S(2)}, u32[]{:S(2)}) collective-permute-start(bf16[288,256]{1,0:T(8,128)(2,1)} %get-tuple-element.65), channel_id=1, source_target_pairs={{2,0},{3,1},{4,6},{5,7},{10,8},{11,9},{12,14},{13,15},{18,16},{19,... | collective-permute-start | bytes 442376 | tf_op jit(solution)/shard_map/ppermute | solution.py:624
  128.9 76.4 %collective-permute-start.17 = (bf16[256,1024]{1,0:T(8,128)(2,1)}, bf16[256,1024]{1,0:T(8,128)(2,1)S(1)}, u32[]{:S(2)}, u32[]{:S(2)}) collective-permute-start(bf16[256,1024]{1,0:T(8,128)(2,1)} %get-tuple-element.69), channel_id=1, source_target_pairs={{2,0},{3,1},{4,6},{5,7},{10,8},{11,9},{12,14},{13,15},{18,16},{19,... | collective-permute-start | bytes 1572872 | tf_op jit(solution)/shard_map/ppermute | solution.py:624
  194.2 12.6 %collective-permute-start.15 = (bf16[288,256]{1,0:T(8,128)(2,1)S(1)}, bf16[288,256]{1,0:T(8,128)(2,1)S(1)}, u32[]{:S(2)}, u32[]{:S(2)}) collective-permute-start(bf16[288,256]{1,0:T(8,128)(2,1)S(1)} %broadcast_select_fusion.4), channel_id=1, source_target_pairs={{0,8},{8,16},{16,24},{24,0},{1,9},{9,17},{17,25},{25,1},{2,10},{10... | collective-permute-start | bytes 442376 | tf_op jit(solution)/shard_map/ppermute | solution.py:630
  198.9 15.7 %collective-permute-start.21 = (bf16[256,1024]{1,0:T(8,128)(2,1)S(1)}, bf16[256,1024]{1,0:T(8,128)(2,1)S(1)}, u32[]{:S(2)}, u32[]{:S(2)}) collective-permute-start(bf16[256,1024]{1,0:T(8,128)(2,1)S(1)} %broadcast_select_fusion), channel_id=1, source_target_pairs={{0,8},{8,16},{16,24},{24,0},{1,9},{9,17},{17,25},{25,1},{2,10},{10... | collective-permute-start | bytes 1572872 | tf_op jit(solution)/shard_map/ppermute | solution.py:630
  205.3 19.0 %collective-permute-start.18 = (bf16[256,1024]{1,0:T(8,128)(2,1)S(1)}, bf16[256,1024]{1,0:T(8,128)(2,1)S(1)}, u32[]{:S(2)}, u32[]{:S(2)}) collective-permute-start(bf16[256,1024]{1,0:T(8,128)(2,1)S(1)} %broadcast_select_fusion.1), channel_id=1, source_target_pairs={{0,8},{8,16},{16,24},{24,0},{1,9},{9,17},{17,25},{25,1},{2,10},{10... | collective-permute-start | bytes 1572872 | tf_op jit(solution)/shard_map/ppermute | solution.py:630
  (14 other events, 265.8 us)
